TPU v7x, 128 devices: a whole 4x4x4 slice. The times are simulated.
128 devices in a mesh: section: 4 (over x_lo, core), rep: 32 (over x_hi, z, y).
Axes of the slice: x: 4 (x_hi: 2, x_lo: 2; x = x_hi * 2 + x_lo), y: 4, z: 4, core: 2. Of those that a mesh axis runs over, the one named last changes fastest.
Arguments:
- x_in: bfloat16 [32, 768, 1024], P('rep'), may hold values from -6 to 6
- cotangent: bfloat16 [32, 768, 1024], P('rep'), may hold values from -6 to 6
- norm_gain: float32 [4, 1024], P('section'), may hold values from 0.1 to 1.9
- w_up: bfloat16 [32, 4, 1024, 2048], P('rep', 'section'), may hold values from -0.1875 to 0.1875
- w_down: bfloat16 [32, 4, 2048, 1024], P('rep', 'section'), may hold values from -0.125 to 0.125
- live: int32 [32], replicated, may hold values from 0 to 1, as said below
- donor: int32 [32], replicated, may hold values from 0 to 31, as said below
Outputs:
- section_out: bfloat16 [32, 4, 768, 1024], P('rep', 'section')
- section_in_grad: bfloat16 [32, 4, 768, 1024], P('rep', 'section')
- grad_up: bfloat16 [32, 4, 1024, 2048], P('rep', 'section')
- grad_down: bfloat16 [32, 4, 2048, 1024], P('rep', 'section')
Inputs may be any that keep to these rules, and one draw needn't show every extreme that they name: At least one replica is dead and at least half are live. `donor`: for a dead replica, the index of a live replica; for a live replica any index, unused.
All inputs are finite; a program needn't handle non-finite values.
Results may differ from a plain program's by a relative error of at most 0.014.
Values may be sent and summed in bfloat16 or wider, within the bound.
No kernel may reach another device: no remote copies, remote signals or barrier semaphores. Data moves between devices by JAX's collectives and lax.ppermute only.
A program may use at most 320 MiB of HBM per device.

v0:
```python
import jax
import jax.numpy as jnp
from jax import lax
from jax.sharding import PartitionSpec as P

ROWS = 192
MICRO = 4


GELU_C = 0.7978845608028654


def split_up(shard, dim, peers):
    before, after = (shard.shape[:dim], shard.shape[dim + 1 :])
    return jnp.moveaxis(shard.reshape(*before, peers, -1, *after), dim, 0)


def edges_of(length, count):
    unit = 8 if length >= 8 * count else 1
    return [length // unit * k // count * unit for k in range(1, count)]


def in_order(parts, dim):
    lengths = list(parts.shape[1:])
    lengths[dim] *= parts.shape[0]
    return jnp.moveaxis(parts, 0, dim).reshape(lengths)


def exchange_in_pieces(shard, axis, pieces, split_dim, concat_dim):
    parts = split_up(shard, split_dim, lax.axis_size(axis))
    widest = max(range(1, max(2, parts.ndim - 1)), key=lambda d: parts.shape[d])
    done = []
    for section in jnp.split(parts, edges_of(parts.shape[widest], pieces), axis=widest):
        if section.size:
            done.append(lax.all_to_all(section, axis, split_axis=0, concat_axis=0, tiled=True))
    return in_order(jnp.concatenate(done, axis=widest), concat_dim)


def shifted(shard, axis, by):
    peers = lax.axis_size(axis)
    pairs = [(i, i + by) for i in range(peers) if 0 <= i + by < peers]
    return lax.ppermute(shard, axis, pairs)


def gelu_value(u):
    inner = jnp.tanh(GELU_C * (u + 0.044715 * u * u * u))
    return 0.5 * u * (1.0 + inner)


def gelu_slope(u):
    inner = jnp.tanh(GELU_C * (u + 0.044715 * u * u * u))
    return 0.5 * (1.0 + inner) + 0.5 * u * (1.0 - inner * inner) * GELU_C * (
        1.0 + 3.0 * 0.044715 * u * u
    )


def contract(left, right, left_dim, right_dim):
    return lax.dot_general(
        left, right, (((left_dim,), (right_dim,)), ((), ())), preferred_element_type=jnp.float32
    )


def norm_components(token_rows):
    values = token_rows.astype(jnp.float32)
    center = values - jnp.mean(values, axis=-1, keepdims=True)
    scale_factor = lax.rsqrt(jnp.mean(center * center, axis=-1, keepdims=True) + 1e-05)
    return (center * scale_factor, scale_factor)


def layer_forward(token_rows, gain_vector, up_proj, down_proj):
    standardized_input, scale_factor = norm_components(token_rows)
    normalized_rows = (standardized_input * gain_vector).astype(jnp.bfloat16)
    pre = contract(normalized_rows, up_proj, 1, 0)
    hidden = gelu_value(pre).astype(jnp.bfloat16)
    out = (token_rows.astype(jnp.float32) + contract(hidden, down_proj, 1, 0)).astype(jnp.bfloat16)
    return (normalized_rows, pre, hidden, out)


def layer_backward(
    token_rows, grad_out, gain_vector, up_proj, down_proj, normalized_rows, pre, hidden
):
    grad_hidden = contract(grad_out, down_proj, 1, 1)
    grad_pre = (grad_hidden * gelu_slope(pre)).astype(jnp.bfloat16)
    step_up = contract(normalized_rows, grad_pre, 0, 0)
    step_down = contract(hidden, grad_out, 0, 0)
    grad_normed = contract(grad_pre, up_proj, 1, 1)
    standardized_input, scale_factor = norm_components(token_rows)
    weighted_rows = grad_normed * gain_vector
    centered_rows = (
        weighted_rows
        - jnp.mean(weighted_rows, axis=-1, keepdims=True)
        - standardized_input * jnp.mean(weighted_rows * standardized_input, axis=-1, keepdims=True)
    )
    grad_in = (grad_out.astype(jnp.float32) + scale_factor * centered_rows).astype(jnp.bfloat16)
    return (grad_in, step_up, step_down)


def store_slot(buffer, value, slot, valid):
    previous = lax.dynamic_index_in_dim(buffer, slot, 0, keepdims=False)
    return lax.dynamic_update_index_in_dim(buffer, jnp.where(valid, value, previous), slot, 0)


def load_slot(buffer, slot):
    return lax.dynamic_index_in_dim(buffer, slot, 0, keepdims=False)


def per_device(x_in, cotangent, norm_gain, w_up, w_down, live, donor):
    member = lax.axis_index("rep")
    level = lax.axis_index("section")
    depth = lax.axis_size("section")
    own_up = w_up[0, 0]
    own_down = w_down[0, 0]
    gain_vector = norm_gain[0]
    held_up, held_down = (
        exchange_in_pieces(own_up[None], "rep", 2, 1, 0),
        exchange_in_pieces(own_down[None], "rep", 2, 1, 0),
    )
    picked_up = jnp.take(held_up, donor, axis=0)
    picked_down = jnp.take(held_down, donor, axis=0)
    back_up, back_down = (
        lax.all_to_all(picked_up, "rep", split_axis=0, concat_axis=1, tiled=True),
        lax.all_to_all(picked_down, "rep", split_axis=0, concat_axis=1, tiled=True),
    )
    alive = live[member] == 1
    used_up = jnp.where(alive, own_up, back_up[0])
    used_down = jnp.where(alive, own_down, back_down[0])
    width = own_up.shape[0]
    hidden_width = own_up.shape[1]
    rounds = MICRO + depth - 1
    inputs_buf = jnp.zeros((MICRO, ROWS, width), jnp.bfloat16)
    outputs_buf = jnp.zeros((MICRO, ROWS, width), jnp.bfloat16)
    normed_buf = jnp.zeros((MICRO, ROWS, width), jnp.bfloat16)
    pre_buf = jnp.zeros((MICRO, ROWS, hidden_width), jnp.float32)
    hidden_buf = jnp.zeros((MICRO, ROWS, hidden_width), jnp.bfloat16)
    arrived = jnp.zeros((ROWS, width), jnp.bfloat16)
    for turn in range(rounds):
        micro_index = turn - level
        valid = (micro_index >= 0) & (micro_index < MICRO)
        slot = jnp.clip(micro_index, 0, MICRO - 1)
        first = lax.dynamic_slice_in_dim(x_in[0], slot * ROWS, ROWS, 0)
        token_rows = jnp.where(level == 0, first, arrived)
        normalized_rows, pre, hidden, out = layer_forward(
            token_rows, gain_vector, used_up, used_down
        )
        inputs_buf = store_slot(inputs_buf, token_rows, slot, valid)
        outputs_buf = store_slot(outputs_buf, out, slot, valid)
        normed_buf = store_slot(normed_buf, normalized_rows, slot, valid)
        pre_buf = store_slot(pre_buf, pre, slot, valid)
        hidden_buf = store_slot(hidden_buf, hidden, slot, valid)
        if turn + 1 < rounds:
            arrived = shifted(out, "section", 1)
    grads_in_buf = jnp.zeros((MICRO, ROWS, width), jnp.bfloat16)
    total_up = jnp.zeros((width, hidden_width), jnp.float32)
    total_down = jnp.zeros((hidden_width, width), jnp.float32)
    arrived = jnp.zeros((ROWS, width), jnp.bfloat16)
    for turn in range(rounds):
        micro_index = turn - (depth - 1 - level)
        valid = (micro_index >= 0) & (micro_index < MICRO)
        slot = jnp.clip(micro_index, 0, MICRO - 1)
        last = lax.dynamic_slice_in_dim(cotangent[0], slot * ROWS, ROWS, 0)
        grad_out = jnp.where(level == depth - 1, last, arrived)
        grad_out = jnp.where(valid, grad_out, jnp.zeros_like(grad_out))
        token_rows = load_slot(inputs_buf, slot)
        normalized_rows = load_slot(normed_buf, slot)
        pre = load_slot(pre_buf, slot)
        hidden = load_slot(hidden_buf, slot)
        grad_in, step_up, step_down = layer_backward(
            token_rows, grad_out, gain_vector, used_up, used_down, normalized_rows, pre, hidden
        )
        total_up = total_up + step_up
        total_down = total_down + step_down
        grads_in_buf = store_slot(grads_in_buf, grad_in, slot, valid)
        if turn + 1 < rounds:
            arrived = shifted(grad_in, "section", -1)
    section_out = outputs_buf.reshape(1, 1, MICRO * ROWS, width)
    section_in_grad = grads_in_buf.reshape(1, 1, MICRO * ROWS, width)
    grad_up = total_up.astype(jnp.bfloat16)[None, None]
    grad_down = total_down.astype(jnp.bfloat16)[None, None]
    return (section_out, section_in_grad, grad_up, grad_down)


def solution(mesh):
    return jax.shard_map(
        per_device,
        mesh=mesh,
        in_specs=(
            P("rep", None, None),
            P("rep", None, None),
            P("section", None),
            P("rep", "section", None, None),
            P("rep", "section", None, None),
            P(),
            P(),
        ),
        out_specs=(
            P("rep", "section", None, None),
            P("rep", "section", None, None),
            P("rep", "section", None, None),
            P("rep", "section", None, None),
        ),
        check_vma=False,
    )
```

profile of v0, /device:TPU:17, one launch (start us, length us, event | category | flops | bytes accessed | tf_op | source)
XLA Modules:
  0.0 547.1 jit_solution(8301341172099819537)
XLA Ops:
  0.6 5.1 fusion.334
  5.7 10.3 %all-to-all-start.3 = ((bf16[32,1,32,1024]{3,2,1,0:T(8,128)(2,1)}), bf16[32,1,32,1024]{3,2,1,0:T(8,128)(2,1)S(1)}, u32[]{:S(2)}, u32[]{:S(2)}) async-start(bf16[32,1,32,1024]{3,2,1,0:T(8,128)(2,1)} %get-tuple-element.57), calls=%async_computation.3 | async-start | bytes 4194304 | tf_op jit(solution)/shard_map/all_to_all | solution.py:35
  16.0 4.9 fusion.333
  20.9 21.6 %all-to-all-done.3 = bf16[32,1,32,1024]{3,2,1,0:T(8,128)(2,1)S(1)} async-done(((bf16[32,1,32,1024]{3,2,1,0:T(8,128)(2,1)}), bf16[32,1,32,1024]{3,2,1,0:T(8,128)(2,1)S(1)}, u32[]{:S(2)}, u32[]{:S(2)}) %all-to-all-start.3) | async-done | bytes 2097184 | tf_op jit(solution)/shard_map/all_to_all | solution.py:35
  42.5 35.8 %all_to_all.38 = bf16[32,1,16,2048]{3,2,1,0:T(8,128)(2,1)} all-to-all(bf16[32,1,16,2048]{3,2,1,0:T(8,128)(2,1)} %get-tuple-element.55), channel_id=1, replica_groups=mesh['section'=4,'rep'=32] {'rep'}, dimensions={0} | all-to-all | bytes 4194304 | tf_op jit(solution)/shard_map/all_to_all | solution.py:35
  78.3 34.2 %all_to_all.39 = bf16[32,1,16,2048]{3,2,1,0:T(8,128)(2,1)} all-to-all(bf16[32,1,16,2048]{3,2,1,0:T(8,128)(2,1)S(1)} %copy-done.6), channel_id=1, replica_groups=mesh['section'=4,'rep'=32] {'rep'}, dimensions={0} | all-to-all | bytes 4194304 | tf_op jit(solution)/shard_map/all_to_all | solution.py:35
  112.5 7.5 %all-to-all-start.4 = ((bf16[32,1,32,1024]{3,2,1,0:T(8,128)(2,1)}), bf16[32,1,32,1024]{3,2,1,0:T(8,128)(2,1)}, u32[]{:S(2)}, u32[]{:S(2)}) async-start(bf16[32,1,32,1024]{3,2,1,0:T(8,128)(2,1)} %get-tuple-element.58), calls=%async_computation.4 | async-start | bytes 4194304 | tf_op jit(solution)/shard_map/all_to_all | solution.py:35
  120.1 4.8 maximum_bitcast_fusion
  124.9 5.0 gather_fusion
  129.9 4.6 broadcast_select_fusion.1
  134.5 11.8 %all-to-all-done.4 = bf16[32,1,32,1024]{3,2,1,0:T(8,128)(2,1)} async-done(((bf16[32,1,32,1024]{3,2,1,0:T(8,128)(2,1)}), bf16[32,1,32,1024]{3,2,1,0:T(8,128)(2,1)}, u32[]{:S(2)}, u32[]{:S(2)}) %all-to-all-start.4) | async-done | bytes 2097184 | tf_op jit(solution)/shard_map/all_to_all | solution.py:35
  146.3 8.9 %all-to-all-start.2 = ((bf16[32,32,2048]{2,1,0:T(8,128)(2,1)}), bf16[32,32,2048]{2,1,0:T(8,128)(2,1)}, u32[]{:S(2)}, u32[]{:S(2)}) async-start(bf16[32,32,2048]{2,1,0:T(8,128)(2,1)} %broadcast_select_fusion.1), calls=%async_computation.2 | async-start | bytes 8388608 | tf_op jit(solution)/shard_map/all_to_all | solution.py:121
  155.2 4.3 maximum_bitcast_fusion.1
  159.5 5.0 gather_fusion.1
  164.5 4.7 broadcast_select_fusion
  169.2 41.3 %all-to-all-done.2 = bf16[32,32,2048]{2,1,0:T(8,128)(2,1)} async-done(((bf16[32,32,2048]{2,1,0:T(8,128)(2,1)}), bf16[32,32,2048]{2,1,0:T(8,128)(2,1)}, u32[]{:S(2)}, u32[]{:S(2)}) %all-to-all-start.2) | async-done | bytes 4194336 | tf_op jit(solution)/shard_map/all_to_all | solution.py:121
  210.5 6.6 %all-to-all-start.5 = ((bf16[32,64,1024]{2,1,0:T(8,128)(2,1)}), bf16[32,64,1024]{2,1,0:T(8,128)(2,1)}, u32[]{:S(2)}, u32[]{:S(2)}) async-start(bf16[32,64,1024]{2,1,0:T(8,128)(2,1)} %broadcast_select_fusion), calls=%async_computation.5 | async-start | bytes 8388608 | tf_op jit(solution)/shard_map/all_to_all | solution.py:122
  219.2 3.4 broadcast_in_dim.219
  222.7 2.4 bitcast_dynamic-update-slice_fusion.6
  225.1 2.2 broadcast_in_dim.241
  228.7 42.5 %all-to-all-done.5 = bf16[32,64,1024]{2,1,0:T(8,128)(2,1)} async-done(((bf16[32,64,1024]{2,1,0:T(8,128)(2,1)}), bf16[32,64,1024]{2,1,0:T(8,128)(2,1)}, u32[]{:S(2)}, u32[]{:S(2)}) %all-to-all-start.5) | async-done | bytes 4194336 | tf_op jit(solution)/shard_map/all_to_all | solution.py:122
  271.1 3.9 bitcast_select_fusion.1
  277.7 6.7 %collective-permute-start = (bf16[192,1024]{1,0:T(8,128)(2,1)S(1)}, bf16[192,1024]{1,0:T(8,128)(2,1)S(1)}, u32[]{:S(2)}, u32[]{:S(2)}) collective-permute-start(bf16[192,1024]{1,0:T(8,128)(2,1)S(1)} %get-tuple-element.61), channel_id=1, source_target_pairs={{0,32},{32,64},{64,96},{1,33},{33,65},{65,97},{2,34},{34,66},{66,9... | collective-permute-start | bytes 1179656 | tf_op jit(solution)/shard_map/ppermute | solution.py:42
  285.6 2.7 bitcast_select_fusion
  290.6 2.3 bitcast_dynamic-update-slice_fusion.5
  295.6 3.3 collective-permute-start.1
  301.7 1.9 collective-permute-done.1
  304.2 2.3 bitcast_dynamic-update-slice_fusion.4
  309.2 4.4 collective-permute-start.2
  319.0 2.3 bitcast_dynamic-update-slice_fusion.3
  324.0 4.8 collective-permute-start.3
  335.6 2.3 bitcast_dynamic-update-slice_fusion.2
  340.6 4.4 collective-permute-start.4
  350.7 2.3 bitcast_dynamic-update-slice_fusion.1
  355.8 4.6 collective-permute-start.5
  366.6 2.3 bitcast_dynamic-update-slice_fusion
  373.6 3.7 fusion.13
  377.3 2.1 fusion.223
  383.0 2.1 collective-permute-start.6
  385.2 5.7 %fusion.243 = f32[2048,1024]{1,0:T(8,128)} fusion(bf16[4,192,2048]{2,1,0:T(8,128)(2,1)} %bitcast_dynamic-update-slice_fusion.7, s32[]{:T(128)S(6)} %min.50, bf16[1,768,1024]{2,1,0:T(8,128)(2,1)S(1)} %copy-done.7, s32[]{:T(128)S(6)} %select_n.576, pred[]{:T(512)S(6)} %eq.12, pred[]{:T(512)S(6)} %and.59), kind=kOutput, calls=%fused_computation.337 | convolution fusion | flops 805699584 | bytes 9568266 | tf_op jit(solution)/shard_map/dot_general | solution.py:58
  390.8 4.5 fusion.266
  395.5 3.5 fusion.16
  399.0 4.5 fusion.264
  407.5 2.3 collective-permute-start.7
  409.8 5.7 %fusion.241 = f32[2048,1024]{1,0:T(8,128)} fusion(bf16[192,1024]{1,0:T(8,128)(2,1)S(1)} %fusion.273, bf16[4,192,2048]{2,1,0:T(8,128)(2,1)} %bitcast_dynamic-update-slice_fusion.7, s32[]{:T(128)S(6)} %min.51), kind=kOutput, calls=%fused_computation.335 | convolution fusion | flops 805306368 | bytes 9568260 | tf_op jit(solution)/shard_map/dot_general | solution.py:58
  417.5 3.5 fusion.17
  421.0 4.5 fusion.262
  429.5 1.9 collective-permute-start.8
  431.4 5.7 %fusion.239 = f32[2048,1024]{1,0:T(8,128)} fusion(bf16[192,1024]{1,0:T(8,128)(2,1)S(1)} %fusion.272, bf16[4,192,2048]{2,1,0:T(8,128)(2,1)} %bitcast_dynamic-update-slice_fusion.7, s32[]{:T(128)S(6)} %min.52), kind=kOutput, calls=%fused_computation.333 | convolution fusion | flops 805306368 | bytes 9568260 | tf_op jit(solution)/shard_map/dot_general | solution.py:58
  438.7 3.5 fusion.18
  442.2 4.6 fusion.260
  450.8 2.1 collective-permute-start.9
  452.9 5.7 %fusion.237 = f32[2048,1024]{1,0:T(8,128)} fusion(bf16[192,1024]{1,0:T(8,128)(2,1)S(1)} %fusion.271, bf16[4,192,2048]{2,1,0:T(8,128)(2,1)} %bitcast_dynamic-update-slice_fusion.7, s32[]{:T(128)S(6)} %min.53), kind=kOutput, calls=%fused_computation.331 | convolution fusion | flops 805306368 | bytes 9568260 | tf_op jit(solution)/shard_map/dot_general | solution.py:58
  460.2 3.5 fusion.19
  463.7 4.5 fusion.258
  472.2 1.9 collective-permute-start.10
  474.1 5.6 %fusion.235 = f32[2048,1024]{1,0:T(8,128)} fusion(bf16[192,1024]{1,0:T(8,128)(2,1)S(1)} %fusion.270, bf16[4,192,2048]{2,1,0:T(8,128)(2,1)} %bitcast_dynamic-update-slice_fusion.7, s32[]{:T(128)S(6)} %min.54), kind=kOutput, calls=%fused_computation.329 | convolution fusion | flops 805306368 | bytes 9568260 | tf_op jit(solution)/shard_map/dot_general | solution.py:58
  481.4 3.5 fusion.20
  485.0 4.6 fusion.256
  493.5 2.1 collective-permute-start.11
  495.7 5.6 %fusion.233 = f32[2048,1024]{1,0:T(8,128)} fusion(bf16[192,1024]{1,0:T(8,128)(2,1)S(1)} %fusion.269, bf16[4,192,2048]{2,1,0:T(8,128)(2,1)} %bitcast_dynamic-update-slice_fusion.7, s32[]{:T(128)S(6)} %min.55), kind=kOutput, calls=%fused_computation.327 | convolution fusion | flops 805306368 | bytes 9568260 | tf_op jit(solution)/shard_map/dot_general | solution.py:58
  502.8 3.6 fusion.21
  509.3 18.4 %fusion.9 = bf16[1,1,1024,2048]{3,2,1,0:T(8,128)(2,1)} fusion(bf16[192,2048]{1,0:T(8,128)(2,1)} %copy-done.10, f32[1024,2048]{1,0:T(8,128)} %fusion.256, f32[1024,2048]{1,0:T(8,128)} %fusion.258, f32[1024,2048]{1,0:T(8,128)} %fusion.260, f32[1024,2048]{1,0:T(8,128)} %fusion.262, f32[1024,2048]{1,0:T(8,128)} %fusion.266, f32[1024,2048]{1,0:T(8,128)} %fusion.264, ...), kind=kOutput, calls=%fused_computation.19 | convolution fusion | flops 819986432 | bytes 55705604 | tf_op jit(solution)/shard_map/dot_general | solution.py:58
  527.7 19.2 %fusion = bf16[1,1,2048,1024]{3,2,1,0:T(8,128)(2,1)} fusion(f32[2048,1024]{1,0:T(8,128)} %fusion.233, f32[2048,1024]{1,0:T(8,128)} %fusion.235, f32[2048,1024]{1,0:T(8,128)} %fusion.237, f32[2048,1024]{1,0:T(8,128)} %fusion.239, f32[2048,1024]{1,0:T(8,128)} %fusion.243, f32[2048,1024]{1,0:T(8,128)} %fusion.241, bf16[192,1024]{1,0:T(8,128)(2,1)S(1)} %fusion.268, ...), kind=kOutput, calls=%fused_computation.4 | convolution fusion | flops 819986432 | bytes 55705604 | tf_op jit(solution)/shard_map/dot_general | solution.py:58
  (186 shorter events, 88.9 us)
Async XLA Ops:
  5.7 36.8 %all-to-all-start.3 = ((bf16[32,1,32,1024]{3,2,1,0:T(8,128)(2,1)}), bf16[32,1,32,1024]{3,2,1,0:T(8,128)(2,1)S(1)}, u32[]{:S(2)}, u32[]{:S(2)}) async-start(bf16[32,1,32,1024]{3,2,1,0:T(8,128)(2,1)} %get-tuple-element.57), calls=%async_computation.3 | async-start | bytes 4194304 | tf_op jit(solution)/shard_map/all_to_all | solution.py:35
  42.5 35.8 %copy-start.6 = (bf16[32,1,16,2048]{3,2,1,0:T(8,128)(2,1)S(1)}, bf16[32,1,16,2048]{3,2,1,0:T(8,128)(2,1)}, u32[]{:S(2)}) copy-start(bf16[32,1,16,2048]{3,2,1,0:T(8,128)(2,1)} %get-tuple-element.56) | copy-start | bytes 6291460
  112.5 7.5 %copy-start.12 = (s32[32]{0:T(128)S(1)}, s32[32]{0:T(128)}, u32[]{:S(2)}) copy-start(s32[32]{0:T(128)} %param.13) | copy-start | bytes 388
  112.5 33.9 %all-to-all-start.4 = ((bf16[32,1,32,1024]{3,2,1,0:T(8,128)(2,1)}), bf16[32,1,32,1024]{3,2,1,0:T(8,128)(2,1)}, u32[]{:S(2)}, u32[]{:S(2)}) async-start(bf16[32,1,32,1024]{3,2,1,0:T(8,128)(2,1)} %get-tuple-element.58), calls=%async_computation.4 | async-start | bytes 4194304 | tf_op jit(solution)/shard_map/all_to_all | solution.py:35
  146.3 64.2 %all-to-all-start.2 = ((bf16[32,32,2048]{2,1,0:T(8,128)(2,1)}), bf16[32,32,2048]{2,1,0:T(8,128)(2,1)}, u32[]{:S(2)}, u32[]{:S(2)}) async-start(bf16[32,32,2048]{2,1,0:T(8,128)(2,1)} %broadcast_select_fusion.1), calls=%async_computation.2 | async-start | bytes 8388608 | tf_op jit(solution)/shard_map/all_to_all | solution.py:121
  169.2 48.1 %copy-start.13 = (s32[32]{0:T(128)S(1)}, s32[32]{0:T(128)}, u32[]{:S(2)}) copy-start(s32[32]{0:T(128)} %param.12) | copy-start | bytes 388
  169.2 49.3 %copy-start.4 = (bf16[1,768,1024]{2,1,0:T(8,128)(2,1)S(1)}, bf16[1,768,1024]{2,1,0:T(8,128)(2,1)}, u32[]{:S(2)}) copy-start(bf16[1,768,1024]{2,1,0:T(8,128)(2,1)} %param.7) | copy-start | bytes 4718596
  210.5 60.6 %all-to-all-start.5 = ((bf16[32,64,1024]{2,1,0:T(8,128)(2,1)}), bf16[32,64,1024]{2,1,0:T(8,128)(2,1)}, u32[]{:S(2)}, u32[]{:S(2)}) async-start(bf16[32,64,1024]{2,1,0:T(8,128)(2,1)} %broadcast_select_fusion), calls=%async_computation.5 | async-start | bytes 8388608 | tf_op jit(solution)/shard_map/all_to_all | solution.py:122
  219.2 3.5 copy-start
  219.2 3.4 copy-start.11
  225.1 2.2 copy-start.8
  275.0 1.4 copy-start.9
  276.5 9.1 %copy-start.1 = (bf16[1,1,1024,2048]{3,2,1,0:T(8,128)(2,1)S(1)}, bf16[1,1,1024,2048]{3,2,1,0:T(8,128)(2,1)}, u32[]{:S(2)}) copy-start(bf16[1,1,1024,2048]{3,2,1,0:T(8,128)(2,1)} %param.10) | copy-start | bytes 12582916
  277.7 12.3 %collective-permute-start = (bf16[192,1024]{1,0:T(8,128)(2,1)S(1)}, bf16[192,1024]{1,0:T(8,128)(2,1)S(1)}, u32[]{:S(2)}, u32[]{:S(2)}) collective-permute-start(bf16[192,1024]{1,0:T(8,128)(2,1)S(1)} %get-tuple-element.61), channel_id=1, source_target_pairs={{0,32},{32,64},{64,96},{1,33},{33,65},{65,97},{2,34},{34,66},{66,9... | collective-permute-start | bytes 1179656 | tf_op jit(solution)/shard_map/ppermute | solution.py:42
  295.6 8.0 %collective-permute-start.1 = (bf16[192,1024]{1,0:T(8,128)(2,1)S(1)}, bf16[192,1024]{1,0:T(8,128)(2,1)S(1)}, u32[]{:S(2)}, u32[]{:S(2)}) collective-permute-start(bf16[192,1024]{1,0:T(8,128)(2,1)S(1)} %get-tuple-element.63), channel_id=1, source_target_pairs={{0,32},{32,64},{64,96},{1,33},{33,65},{65,97},{2,34},{34,66},{66,9... | collective-permute-start | bytes 1179656 | tf_op jit(solution)/shard_map/ppermute | solution.py:42
  309.2 9.1 %collective-permute-start.2 = (bf16[192,1024]{1,0:T(8,128)(2,1)S(1)}, bf16[192,1024]{1,0:T(8,128)(2,1)S(1)}, u32[]{:S(2)}, u32[]{:S(2)}) collective-permute-start(bf16[192,1024]{1,0:T(8,128)(2,1)S(1)} %get-tuple-element.65), channel_id=1, source_target_pairs={{0,32},{32,64},{64,96},{1,33},{33,65},{65,97},{2,34},{34,66},{66,9... | collective-permute-start | bytes 1179656 | tf_op jit(solution)/shard_map/ppermute | solution.py:42
  324.0 9.1 %collective-permute-start.3 = (bf16[192,1024]{1,0:T(8,128)(2,1)S(1)}, bf16[192,1024]{1,0:T(8,128)(2,1)S(1)}, u32[]{:S(2)}, u32[]{:S(2)}) collective-permute-start(bf16[192,1024]{1,0:T(8,128)(2,1)S(1)} %get-tuple-element.67), channel_id=1, source_target_pairs={{0,32},{32,64},{64,96},{1,33},{33,65},{65,97},{2,34},{34,66},{66,9... | collective-permute-start | bytes 1179656 | tf_op jit(solution)/shard_map/ppermute | solution.py:42
  331.6 1.7 copy-start.5
  340.6 9.1 %collective-permute-start.4 = (bf16[192,1024]{1,0:T(8,128)(2,1)S(1)}, bf16[192,1024]{1,0:T(8,128)(2,1)S(1)}, u32[]{:S(2)}, u32[]{:S(2)}) collective-permute-start(bf16[192,1024]{1,0:T(8,128)(2,1)S(1)} %get-tuple-element.69), channel_id=1, source_target_pairs={{0,32},{32,64},{64,96},{1,33},{33,65},{65,97},{2,34},{34,66},{66,9... | collective-permute-start | bytes 1179656 | tf_op jit(solution)/shard_map/ppermute | solution.py:42
  355.8 9.1 %collective-permute-start.5 = (bf16[192,1024]{1,0:T(8,128)(2,1)S(1)}, bf16[192,1024]{1,0:T(8,128)(2,1)S(1)}, u32[]{:S(2)}, u32[]{:S(2)}) collective-permute-start(bf16[192,1024]{1,0:T(8,128)(2,1)S(1)} %get-tuple-element.71), channel_id=1, source_target_pairs={{0,32},{32,64},{64,96},{1,33},{33,65},{65,97},{2,34},{34,66},{66,9... | collective-permute-start | bytes 1179656 | tf_op jit(solution)/shard_map/ppermute | solution.py:42
  370.4 2.2 copy-start.2
  370.4 3.2 copy-start.7
  371.6 5.7 %copy-start.3 = (bf16[4,192,1024]{2,1,0:T(8,128)(2,1)}, bf16[4,192,1024]{2,1,0:T(8,128)(2,1)S(1)}, u32[]{:S(2)}) copy-start(bf16[4,192,1024]{2,1,0:T(8,128)(2,1)S(1)} %fusion.115) | copy-start | bytes 4718596
  383.0 12.3 %collective-permute-start.6 = (bf16[192,1024]{1,0:T(8,128)(2,1)S(1)}, bf16[192,1024]{1,0:T(8,128)(2,1)S(1)}, u32[]{:S(2)}, u32[]{:S(2)}) collective-permute-start(bf16[192,1024]{1,0:T(8,128)(2,1)S(1)} %get-tuple-element.42), channel_id=1, source_target_pairs={{32,0},{64,32},{96,64},{33,1},{65,33},{97,65},{34,2},{66,34},{98,6... | collective-permute-start | bytes 1179656 | tf_op jit(solution)/shard_map/ppermute | solution.py:42
  407.5 9.8 %collective-permute-start.7 = (bf16[192,1024]{1,0:T(8,128)(2,1)S(1)}, bf16[192,1024]{1,0:T(8,128)(2,1)S(1)}, u32[]{:S(2)}, u32[]{:S(2)}) collective-permute-start(bf16[192,1024]{1,0:T(8,128)(2,1)S(1)} %get-tuple-element.40), channel_id=1, source_target_pairs={{32,0},{64,32},{96,64},{33,1},{65,33},{97,65},{34,2},{66,34},{98,6... | collective-permute-start | bytes 1179656 | tf_op jit(solution)/shard_map/ppermute | solution.py:42
  429.5 9.1 %collective-permute-start.8 = (bf16[192,1024]{1,0:T(8,128)(2,1)S(1)}, bf16[192,1024]{1,0:T(8,128)(2,1)S(1)}, u32[]{:S(2)}, u32[]{:S(2)}) collective-permute-start(bf16[192,1024]{1,0:T(8,128)(2,1)S(1)} %get-tuple-element.38), channel_id=1, source_target_pairs={{32,0},{64,32},{96,64},{33,1},{65,33},{97,65},{34,2},{66,34},{98,6... | collective-permute-start | bytes 1179656 | tf_op jit(solution)/shard_map/ppermute | solution.py:42
  450.8 9.2 %collective-permute-start.9 = (bf16[192,1024]{1,0:T(8,128)(2,1)S(1)}, bf16[192,1024]{1,0:T(8,128)(2,1)S(1)}, u32[]{:S(2)}, u32[]{:S(2)}) collective-permute-start(bf16[192,1024]{1,0:T(8,128)(2,1)S(1)} %get-tuple-element.36), channel_id=1, source_target_pairs={{32,0},{64,32},{96,64},{33,1},{65,33},{97,65},{34,2},{66,34},{98,6... | collective-permute-start | bytes 1179656 | tf_op jit(solution)/shard_map/ppermute | solution.py:42
  472.2 9.1 %collective-permute-start.10 = (bf16[192,1024]{1,0:T(8,128)(2,1)S(1)}, bf16[192,1024]{1,0:T(8,128)(2,1)S(1)}, u32[]{:S(2)}, u32[]{:S(2)}) collective-permute-start(bf16[192,1024]{1,0:T(8,128)(2,1)S(1)} %get-tuple-element.34), channel_id=1, source_target_pairs={{32,0},{64,32},{96,64},{33,1},{65,33},{97,65},{34,2},{66,34},{98,6... | collective-permute-start | bytes 1179656 | tf_op jit(solution)/shard_map/ppermute | solution.py:42
  493.5 9.1 %collective-permute-start.11 = (bf16[192,1024]{1,0:T(8,128)(2,1)S(1)}, bf16[192,1024]{1,0:T(8,128)(2,1)S(1)}, u32[]{:S(2)}, u32[]{:S(2)}) collective-permute-start(bf16[192,1024]{1,0:T(8,128)(2,1)S(1)} %get-tuple-element.32), channel_id=1, source_target_pairs={{32,0},{64,32},{96,64},{33,1},{65,33},{97,65},{34,2},{66,34},{98,6... | collective-permute-start | bytes 1179656 | tf_op jit(solution)/shard_map/ppermute | solution.py:42
  506.3 1.7 copy-start.10
where the time goes:
time: 557 us; the launch traced here: 547 us
  matrix products  161 us (29%)
  waiting for transfers between devices  134 us (24%)
  starting transfers between devices  74 us (13%)
  blocking collectives  70 us (13%)
  local copies, waits for them, and re-layouts  54.3 us (10%)
  other arithmetic  51.6 us (9%)
    dot_general x42, matrix products, contract(): lax.dot_general(left, right, (((left_dim,), (right_dim,)), ((), ())), pre...  161 us
    all_to_all x2, blocking collectives, exchange_in_pieces(): lax.all_to_all(section, axis, split_axis=0, concat_axis=0, tiled=True)  70 us
    all_to_all x1, waiting for transfers between devices, per_device(): lax.all_to_all(picked_down, 'rep', split_axis=0, concat_axis=1, tiled=True)  42.5 us
    all_to_all x1, waiting for transfers between devices, per_device(): lax.all_to_all(picked_up, 'rep', split_axis=0, concat_axis=1, tiled=True)  41.3 us
    ppermute x12, starting transfers between devices, shifted(): return lax.ppermute(shard, axis, pairs)  40.7 us
    all_to_all x2, waiting for transfers between devices, exchange_in_pieces(): lax.all_to_all(section, axis, split_axis=0, concat_axis=0, tiled=True)  33.5 us
    dynamic_slice x35, local copies, waits for them, and re-layouts, store_slot(): previous = lax.dynamic_index_in_dim(buffer, slot, 0, keepdims=False)  23 us
    dynamic_update_slice x27, other arithmetic, store_slot(): lax.dynamic_update_index_in_dim(buffer, jnp.where(valid, value, previous)...  22.1 us
  transfers between devices with their start and end apart: 16, of which 14 were waited for; matrix products, arithmetic and copies ran while one was open for 19% of the time, Pallas kernels for 0%

commit v1 on v0

v1 whole, which is shorter than its diff:
```python
import functools

import jax
import jax.numpy as jnp
from jax import lax
from jax.experimental import pallas as pl
from jax.experimental.pallas import tpu as pltpu
from jax.sharding import PartitionSpec as P

MICRO = 4
CHUNK = 512
LAG_FAST = 2
LAG_SLOW = 3
GELU_C = 0.7978845608028654
VMEM_LIMIT = 40 * 1024 * 1024


def row_stats(values):
    center = values - jnp.mean(values, axis=-1, keepdims=True)
    factor = lax.rsqrt(jnp.mean(center * center, axis=-1, keepdims=True) + 1e-05)
    return center * factor, factor


def mm(left, right, left_dim, right_dim):
    return lax.dot_general(
        left, right, (((left_dim,), (right_dim,)), ((), ())), preferred_element_type=jnp.float32
    )


def choose(level, sources):
    value = sources[-1][1][...]
    for levels, ref in sources[:-1]:
        hit = functools.reduce(jnp.logical_or, [level == k for k in levels])
        value = jnp.where(hit, ref[...], value)
    return value


def forward_body(levels_of, meta, *refs):
    n_src = len(levels_of)
    sources = list(zip(levels_of, refs[:n_src]))
    gain, up, down = refs[n_src : n_src + 3]
    send, rows_out, normed_out, hidden_out, slope_out, out = refs[n_src + 8 : n_src + 14]
    normed_s, acc = refs[n_src + 14 :]
    step = pl.program_id(0)
    last = pl.num_programs(0) - 1

    @pl.when(meta[1] == 1)
    def _():
        @pl.when(step == 0)
        def _():
            rows = choose(meta[2], sources)
            rows_out[...] = rows
            xhat, _ = row_stats(rows.astype(jnp.float32))
            normed = (xhat * gain[...]).astype(jnp.bfloat16)
            normed_s[...] = normed
            normed_out[...] = normed
            acc[...] = rows.astype(jnp.float32)

        u = mm(normed_s[...], up[...], 1, 0)
        inner = jnp.tanh(GELU_C * (u + 0.044715 * u * u * u))
        half = 0.5 * (1.0 + inner)
        hidden = (u * half).astype(jnp.bfloat16)
        slope = half + 0.5 * u * (1.0 - inner * inner) * GELU_C * (1.0 + 3.0 * 0.044715 * u * u)
        hidden_out[...] = hidden
        slope_out[...] = slope.astype(jnp.bfloat16)
        acc[...] += mm(hidden, down[...], 1, 0)

        @pl.when(step == last)
        def _():
            result = acc[...].astype(jnp.bfloat16)
            send[...] = result
            out[...] = result


def backward_body(levels_of, meta, *refs):
    n_src = len(levels_of)
    sources = list(zip(levels_of, refs[:n_src]))
    gain, up, down, rows, slope = refs[n_src : n_src + 5]
    send, grad_out, pre_out, grad_in = refs[n_src + 8 : n_src + 12]
    grad_s, acc = refs[n_src + 12 :]
    step = pl.program_id(0)
    last = pl.num_programs(0) - 1

    @pl.when(meta[1] == 1)
    def _():
        @pl.when(step == 0)
        def _():
            grad = choose(meta[2], sources)
            grad_s[...] = grad
            grad_out[...] = grad
            acc[...] = jnp.zeros_like(acc)

        grad_hidden = mm(grad_s[...], down[...], 1, 1)
        grad_pre = (grad_hidden * slope[...].astype(jnp.float32)).astype(jnp.bfloat16)
        pre_out[...] = grad_pre
        acc[...] += mm(grad_pre, up[...], 1, 1)

        @pl.when(step == last)
        def _():
            xhat, factor = row_stats(rows[...].astype(jnp.float32))
            q = acc[...] * gain[...]
            centered = (
                q
                - jnp.mean(q, axis=-1, keepdims=True)
                - xhat * jnp.mean(q * xhat, axis=-1, keepdims=True)
            )
            result = (grad_s[...].astype(jnp.float32) + factor * centered).astype(jnp.bfloat16)
            send[...] = result
            grad_in[...] = result


def source_spec(kind, m, width):
    if kind == "slot":
        return pl.BlockSpec((m, width), lambda j, meta: (jnp.minimum(meta[0], MICRO - 1), 0))
    return pl.BlockSpec((m, width), lambda j, meta: (0, 0))


def stage(body, name, meta, sources, weights, reads, stash, m, flops):
    gain, up, down = weights
    width, hidden = up.shape
    steps = hidden // CHUNK

    def live(j, meta):
        return jnp.where(meta[1] == 1, j, 0)

    def slot_spec(array):
        if array.shape[1] == hidden:
            return pl.BlockSpec((m, CHUNK), lambda j, meta: (meta[0], j))
        return pl.BlockSpec((m, width), lambda j, meta: (meta[0], 0))

    def read_spec(array):
        if array.shape[1] == hidden:
            return pl.BlockSpec((m, CHUNK), lambda j, meta: (meta[0], live(j, meta)))
        return pl.BlockSpec((m, width), lambda j, meta: (meta[0], 0))

    in_specs = [source_spec(kind, m, width) for _, kind, _ in sources]
    in_specs += [
        pl.BlockSpec((1, width), lambda j, meta: (0, 0)),
        pl.BlockSpec((width, CHUNK), lambda j, meta: (0, live(j, meta))),
        pl.BlockSpec((CHUNK, width), lambda j, meta: (live(j, meta), 0)),
    ]
    in_specs += [read_spec(a) for a in reads]
    n_before = len(in_specs)
    in_specs += [pl.BlockSpec(memory_space=pl.ANY) for _ in stash]
    out_specs = [pl.BlockSpec((m, width), lambda j, meta: (0, 0))]
    out_specs += [slot_spec(a) for a in stash]
    outs = [jax.ShapeDtypeStruct((m, width), jnp.bfloat16)]
    outs += [jax.ShapeDtypeStruct(a.shape, a.dtype) for a in stash]
    call = pl.pallas_call(
        functools.partial(body, [levels for levels, _, _ in sources]),
        grid_spec=pltpu.PrefetchScalarGridSpec(
            num_scalar_prefetch=1,
            grid=(steps,),
            in_specs=in_specs,
            out_specs=out_specs,
            scratch_shapes=[
                pltpu.VMEM((m, width), jnp.bfloat16),
                pltpu.VMEM((m, width), jnp.float32),
            ],
        ),
        out_shape=outs,
        input_output_aliases={1 + n_before + i: 1 + i for i in range(len(stash))},
        compiler_params=pltpu.CompilerParams(
            dimension_semantics=("arbitrary",), vmem_limit_bytes=VMEM_LIMIT
        ),
        cost_estimate=pl.CostEstimate(
            flops=flops, bytes_accessed=2 * 2 * width * hidden, transcendentals=0
        ),
        name=name,
    )
    result = call(meta, *[a for _, _, a in sources], gain, up, down, *reads, *stash)
    return result[0], list(result[1:])


def relay(body, name, entry, offsets, direction, level, weights, reads, stash, m):
    depth = len(offsets)
    width, hidden = weights[1].shape
    flops = 4 * m * width * hidden
    rounds = max(offsets) + MICRO
    sent = {}
    head = 0 if direction > 0 else depth - 1
    table = jnp.asarray(offsets, jnp.int32)
    offset = table[level]
    for turn in range(rounds):
        active = [s for s in range(depth) if 0 <= turn - offsets[s] < MICRO]
        index = turn - offset
        valid = (index >= 0) & (index < MICRO)
        slot = jnp.where(valid, index, MICRO)
        meta = jnp.stack([slot, valid.astype(jnp.int32), level]).astype(jnp.int32)
        by_array = {}
        for s in active:
            key = None if s == head else (s - direction, turn - (offsets[s] - offsets[s - direction]))
            array_key = "entry" if key is None else sent[key][0]
            by_array.setdefault(array_key, []).append(s)
        sources = []
        for array_key, levels in by_array.items():
            if array_key == "entry":
                sources.append((levels, "slot", entry))
            else:
                sources.append((levels, "whole", arrays[array_key]))
        send, stash = stage(body, name, meta, sources, weights, reads, stash, m, flops)
        groups = {}
        for s in active:
            if 0 <= s + direction < depth:
                lag = offsets[s + direction] - offsets[s]
                groups.setdefault(lag, []).append(s)
        for lag, members in groups.items():
            moved = lax.ppermute(send, "section", [(s, s + direction) for s in members])
            if turn == 0:
                arrays = {}
            arrays[(turn, lag)] = moved
            for s in members:
                sent[(s, turn)] = ((turn, lag),)
    return stash


def per_device(x_in, cotangent, norm_gain, w_up, w_down, live, donor):
    member = lax.axis_index("rep")
    level = lax.axis_index("section")
    depth = lax.axis_size("section")
    peers = lax.axis_size("rep")
    own_up = w_up[0, 0]
    own_down = w_down[0, 0]
    width, hidden_width = own_up.shape
    tokens = x_in.shape[1]
    m = tokens // MICRO

    def spread(own):
        return lax.all_to_all(
            own.reshape(peers, -1, own.shape[1]), "rep", split_axis=0, concat_axis=0, tiled=True
        )

    def collect(pieces):
        picked = pieces.at[donor].get(mode="promise_in_bounds")
        back = lax.all_to_all(picked, "rep", split_axis=0, concat_axis=0, tiled=True)
        return back.reshape(-1, back.shape[-1])

    alive = live[member] == 1
    held_up = spread(own_up)
    held_down = spread(own_down)
    used_up = jnp.where(alive, own_up, collect(held_up))
    used_down = jnp.where(alive, own_down, collect(held_down))
    weights = (norm_gain, used_up, used_down)

    def space(columns):
        return jnp.zeros(((MICRO + 1) * m, columns), jnp.bfloat16)

    lags = [LAG_SLOW if s % 2 else LAG_FAST for s in range(depth - 1)]
    offsets = [sum(lags[:s]) for s in range(depth)]
    rows, normed, hidden, slope, outs = relay(
        forward_body, "section_forward", x_in[0], offsets, 1, level, weights, [],
        [space(width), space(width), space(hidden_width), space(hidden_width), space(width)], m,
    )
    grads, pres, grads_in = relay(
        backward_body, "section_backward", cotangent[0], offsets[::-1], -1, level, weights,
        [rows, slope], [space(width), space(hidden_width), space(width)], m,
    )
    grad_up = mm(normed[:tokens], pres[:tokens], 0, 0).astype(jnp.bfloat16)
    grad_down = mm(hidden[:tokens], grads[:tokens], 0, 0).astype(jnp.bfloat16)
    return (
        outs[:tokens][None, None],
        grads_in[:tokens][None, None],
        grad_up[None, None],
        grad_down[None, None],
    )


def solution(mesh):
    return jax.shard_map(
        per_device,
        mesh=mesh,
        in_specs=(
            P("rep", None, None),
            P("rep", None, None),
            P("section", None),
            P("rep", "section", None, None),
            P("rep", "section", None, None),
            P(),
            P(),
        ),
        out_specs=(
            P("rep", "section", None, None),
            P("rep", "section", None, None),
            P("rep", "section", None, None),
            P("rep", "section", None, None),
        ),
        check_vma=False,
    )
```

time: 557 us -> 554 us (level)
  the two profiles are of different devices: /device:TPU:17 before, /device:TPU:5 now
where the time goes in v1:
time: 554 us; the launch traced here: 543 us
  waiting for transfers between devices  157 us (28%)
  local copies, waits for them, and re-layouts  125 us (23%)
  Pallas kernels  109 us (20%)
  blocking collectives  59.3 us (11%)
  starting transfers between devices  55.1 us (10%)
  between operations  14.7 us (3%)
  other arithmetic  13.4 us (2%)
  matrix products  10.1 us (2%)
    pallas_call x22, Pallas kernels, stage(): call(meta, *[a for _, _, a in sources], gain, up, down, *reads, *stash)  109 us
    unnamed x152, local copies, waits for them, and re-layouts  107 us
    all_to_all x2, waiting for transfers between devices, collect(): lax.all_to_all(picked, 'rep', split_axis=0, concat_axis=0, tiled=True)  95.9 us
    all_to_all x1, blocking collectives, spread(): lax.all_to_all(own.reshape(peers, -1, own.shape[1]), 'rep', split_axis=0,...  59.3 us
    all_to_all x1, waiting for transfers between devices, spread(): lax.all_to_all(own.reshape(peers, -1, own.shape[1]), 'rep', split_axis=0,...  49.9 us
    ppermute x24, starting transfers between devices, relay(): moved = lax.ppermute(send, 'section', [(s, s + direction) for s in members])  31.5 us
    all_to_all x2, starting transfers between devices, collect(): lax.all_to_all(picked, 'rep', split_axis=0, concat_axis=0, tiled=True)  15.4 us
  transfers between devices with their start and end apart: 27, of which 4 were waited for; matrix products, arithmetic and copies ran while one was open for 4% of the time, Pallas kernels for 18%

profile of v1, /device:TPU:5, one launch (start us, length us, event | category | flops | bytes accessed | tf_op | source)
XLA Modules:
  0.0 543.5 jit_solution(534172089420266728)
XLA Ops:
  0.6 59.3 %all_to_all.20 = bf16[32,32,2048]{2,1,0:T(8,128)(2,1)} all-to-all(bf16[32,32,2048]{2,1,0:T(8,128)(2,1)} %bitcast.96), channel_id=1, replica_groups=mesh['section'=4,'rep'=32] {'rep'}, dimensions={0} | all-to-all | bytes 8388608 | tf_op jit(solution)/shard_map/all_to_all | solution.py:229
  59.9 8.2 %all-to-all-start.2 = ((bf16[32,64,1024]{2,1,0:T(8,128)(2,1)}), bf16[32,64,1024]{2,1,0:T(8,128)(2,1)}, u32[]{:S(2)}, u32[]{:S(2)}) async-start(bf16[32,64,1024]{2,1,0:T(8,128)(2,1)} %bitcast.97), calls=%async_computation.2 | async-start | bytes 8388608 | tf_op jit(solution)/shard_map/all_to_all | solution.py:229
  68.2 5.0 gather_fusion
  73.2 49.9 %all-to-all-done.2 = bf16[32,64,1024]{2,1,0:T(8,128)(2,1)} async-done(((bf16[32,64,1024]{2,1,0:T(8,128)(2,1)}), bf16[32,64,1024]{2,1,0:T(8,128)(2,1)}, u32[]{:S(2)}, u32[]{:S(2)}) %all-to-all-start.2) | async-done | bytes 4194336 | tf_op jit(solution)/shard_map/all_to_all | solution.py:229
  123.1 7.0 %all-to-all-start.1 = ((bf16[32,32,2048]{2,1,0:T(8,128)(2,1)}), bf16[32,32,2048]{2,1,0:T(8,128)(2,1)}, u32[]{:S(2)}, u32[]{:S(2)}) async-start(bf16[32,32,2048]{2,1,0:T(8,128)(2,1)} %gather_fusion), calls=%async_computation.1 | async-start | bytes 8388608 | tf_op jit(solution)/shard_map/all_to_all | solution.py:235
  130.1 5.0 gather_fusion.1
  135.1 49.2 %all-to-all-done.1 = bf16[32,32,2048]{2,1,0:T(8,128)(2,1)} async-done(((bf16[32,32,2048]{2,1,0:T(8,128)(2,1)}), bf16[32,32,2048]{2,1,0:T(8,128)(2,1)}, u32[]{:S(2)}, u32[]{:S(2)}) %all-to-all-start.1) | async-done | bytes 4194336 | tf_op jit(solution)/shard_map/all_to_all | solution.py:235
  184.3 8.4 %all-to-all-start.3 = ((bf16[32,64,1024]{2,1,0:T(8,128)(2,1)}), bf16[32,64,1024]{2,1,0:T(8,128)(2,1)}, u32[]{:S(2)}, u32[]{:S(2)}) async-start(bf16[32,64,1024]{2,1,0:T(8,128)(2,1)} %gather_fusion.1), calls=%async_computation.3 | async-start | bytes 8388608 | tf_op jit(solution)/shard_map/all_to_all | solution.py:235
  195.8 5.9 %bitcast_select_fusion.1.refs_2_.refs_3_ = bf16[1024,2048]{1,0:T(8,128)(2,1)} fusion(bf16[32,32,2048]{2,1,0:T(8,128)(2,1)} %all-to-all-done.1, bf16[1,1,1024,2048]{3,2,1,0:T(8,128)(2,1)} %param.12, pred[]{:T(512)} %bitcast.17), kind=kLoop, calls=%fused_computation.3 | loop fusion | flops 2097152 | bytes 12582913 | tf_op jit(solution)/shard_map/jit(_where)/select_n | solution.py:241
  201.7 46.7 %all-to-all-done.3 = bf16[32,64,1024]{2,1,0:T(8,128)(2,1)} async-done(((bf16[32,64,1024]{2,1,0:T(8,128)(2,1)}), bf16[32,64,1024]{2,1,0:T(8,128)(2,1)}, u32[]{:S(2)}, u32[]{:S(2)}) %all-to-all-start.3) | async-done | bytes 4194336 | tf_op jit(solution)/shard_map/all_to_all | solution.py:235
  248.5 5.9 %bitcast_select_fusion.refs_3_.refs_4_ = bf16[2048,1024]{1,0:T(8,128)(2,1)} fusion(bf16[32,64,1024]{2,1,0:T(8,128)(2,1)} %all-to-all-done.3, bf16[1,1,2048,1024]{3,2,1,0:T(8,128)(2,1)} %param.13, pred[]{:T(512)} %bitcast.17), kind=kLoop, calls=%fused_computation.2 | loop fusion | flops 2097152 | bytes 12582913 | tf_op jit(solution)/shard_map/jit(_where)/select_n | solution.py:242
  255.4 2.4 broadcast_4_refs_6__refs_7_.2.clone.1.refs_7_
  258.1 3.8 section_forward.11
  263.1 3.8 section_forward.12
  266.9 1.9 copy-done.9
  274.7 2.1 copy-done.10
  279.9 7.8 %section_forward.13 = (bf16[192,1024]{1,0:T(8,128)(2,1)}, bf16[960,1024]{1,0:T(8,128)(2,1)S(1)}, bf16[960,1024]{1,0:T(8,128)(2,1)S(1)}, bf16[960,2048]{1,0:T(8,1...) custom-call(s32[3]{0:T(128)S(1)} %add_add_fusion.6.meta, ...), custom_call_target="tpu_custom_call", output_to_operand_aliasing={{1}: (6, {}), {2}: (7, {}), {3}: (8, {}), {4}: (9, {}), {5}... | custom-call | flops 1610612736 | bytes 8388608 | tf_op jit(solution)/shard_map/section_forward/pallas_call | solution.py:171
  287.7 3.9 collective-permute-start.3
  292.9 7.8 %section_forward.14 = (bf16[192,1024]{1,0:T(8,128)(2,1)}, bf16[960,1024]{1,0:T(8,128)(2,1)S(1)}, bf16[960,1024]{1,0:T(8,128)(2,1)S(1)}, bf16[960,2048]{1,0:T(8,1...) custom-call(s32[3]{0:T(128)S(1)} %add_add_fusion.3.meta, ...), custom_call_target="tpu_custom_call", output_to_operand_aliasing={{1}: (6, {}), {2}: (7, {}), {3}: (8, {}), {4}: (9, {}), {5}... | custom-call | flops 1610612736 | bytes 8388608 | tf_op jit(solution)/shard_map/section_forward/pallas_call | solution.py:171
  300.7 1.9 copy-done.11
  309.3 2.1 copy-done
  311.4 2.1 copy-done.12
  316.6 7.7 %section_forward.15 = (bf16[192,1024]{1,0:T(8,128)(2,1)}, bf16[960,1024]{1,0:T(8,128)(2,1)S(1)}, bf16[960,1024]{1,0:T(8,128)(2,1)S(1)}, bf16[960,2048]{1,0:T(8,1...) custom-call(s32[3]{0:T(128)S(1)} %add_add_fusion.7.meta, ...), custom_call_target="tpu_custom_call", output_to_operand_aliasing={{1}: (5, {}), {2}: (6, {}), {3}: (7, {}), {4}: (8, {}), {5}... | custom-call | flops 1610612736 | bytes 8388608 | tf_op jit(solution)/shard_map/section_forward/pallas_call | solution.py:171
  324.3 1.9 copy-done.1
  327.8 7.8 %section_forward.16 = (bf16[192,1024]{1,0:T(8,128)(2,1)}, bf16[960,1024]{1,0:T(8,128)(2,1)S(1)}, bf16[960,1024]{1,0:T(8,128)(2,1)S(1)}, bf16[960,2048]{1,0:T(8,1...) custom-call(s32[3]{0:T(128)S(1)} %add_add_fusion.2.meta, ...), custom_call_target="tpu_custom_call", output_to_operand_aliasing={{1}: (6, {}), {2}: (7, {}), {3}: (8, {}), {4}: (9, {}), {5}... | custom-call | flops 1610612736 | bytes 8388608 | tf_op jit(solution)/shard_map/section_forward/pallas_call | solution.py:171
  337.6 2.1 copy-done.2
  339.7 3.1 section_forward.17
  342.8 1.9 copy-done.3
  344.7 1.9 copy-done.13
  351.9 2.1 copy-done.14
  357.1 3.8 section_forward.18
  361.6 3.7 section_forward.19
  373.6 2.1 copy-done.4
  375.7 2.1 copy-done.16
  380.9 3.1 section_forward.20
  384.0 3.1 section_forward.21
  387.1 1.9 copy-done.17
  393.1 3.1 section_backward.11
  397.6 3.1 section_backward.12
  400.7 2.0 copy-done.19
  408.7 2.1 copy-done.20
  413.9 3.2 section_backward.13
  420.0 3.2 section_backward.14
  423.3 2.0 copy-done.21
  431.7 2.1 copy-done.6
  433.9 2.1 copy-done.22
  439.1 3.2 section_backward.15
  442.3 2.0 copy-done.23
  445.6 2.1 copy-done.24
  449.3 8.7 %section_backward.16 = (bf16[192,1024]{1,0:T(8,128)(2,1)}, bf16[960,1024]{1,0:T(8,128)(2,1)S(1)}, bf16[960,2048]{1,0:T(8,128)(2,1)S(1)}, bf16[960,1024]{1,0:T(8,128)(2,1)S(1)}) custom-call(s32[3]{0:T(128)S(1)} %add_add_fusion.18.meta, bf16[192,1024]{1,0:T(8,128)(2,1)} %collective-permute-done.15.refs_0_, ...), custom_call_target="tpu_custom_call", output_to_operand_aliasing={{1}: (8, {}), {2}: (9, {}), {3}: (10, {})} | custom-call | flops 1610612736 | bytes 8388608 | tf_op jit(solution)/shard_map/section_backward/pallas_call | solution.py:171
  458.0 2.0 copy-done.25
  463.9 2.1 copy-done.26
  466.0 8.0 %section_backward.17 = (bf16[192,1024]{1,0:T(8,128)(2,1)}, bf16[960,1024]{1,0:T(8,128)(2,1)S(1)}, bf16[960,2048]{1,0:T(8,128)(2,1)S(1)}, bf16[960,1024]{1,0:T(8,128)(2,1)S(1)}) custom-call(s32[3]{0:T(128)S(1)} %add_add_fusion.13.meta, ...), custom_call_target="tpu_custom_call", output_to_operand_aliasing={{1}: (7, {}), {2}: (8, {}), {3}: (9, {})} | custom-call | flops 1610612736 | bytes 8388608 | tf_op jit(solution)/shard_map/section_backward/pallas_call | solution.py:171
  474.0 2.0 copy-done.27
  481.3 10.6 %collective-permute-done.21.refs_1_ = bf16[192,1024]{1,0:T(8,128)(2,1)S(1)} collective-permute-done((bf16[192,1024]{1,0:T(8,128)(2,1)}, bf16[192,1024]{1,0:T(8,128)(2,1)S(1)}, u32[]{:S(2)}, u32[]{:S(2)}) %collective-permute-start.21) | collective-permute-done | bytes 393248 | tf_op jit(solution)/shard_map/ppermute | solution.py:208
  491.9 2.1 copy-done.28
  497.1 7.3 %section_backward.18 = (bf16[192,1024]{1,0:T(8,128)(2,1)S(1)}, bf16[960,1024]{1,0:T(8,128)(2,1)S(1)}, bf16[960,2048]{1,0:T(8,128)(2,1)S(1)}, bf16[960,1024]{1,0:T(8,128)(2,1)S(1)}) custom-call(s32[3]{0:T(128)S(1)} %add_add_fusion.20.meta, ...), custom_call_target="tpu_custom_call", output_to_operand_aliasing={{1}: (8, {}), {2}: (9, {}), {3}: (10, {})} | custom-call | flops 1610612736 | bytes 8388608 | tf_op jit(solution)/shard_map/section_backward/pallas_call | solution.py:171
  508.6 7.6 %section_backward.19 = (bf16[192,1024]{1,0:T(8,128)(2,1)S(1)}, bf16[960,1024]{1,0:T(8,128)(2,1)S(1)}, bf16[960,2048]{1,0:T(8,128)(2,1)S(1)}, bf16[960,1024]{1,0:T(8,128)(2,1)S(1)}) custom-call(s32[3]{0:T(128)S(1)} %add_add_fusion.12.meta, ...), custom_call_target="tpu_custom_call", output_to_operand_aliasing={{1}: (8, {}), {2}: (9, {}), {3}: (10, {})} | custom-call | flops 1610612736 | bytes 8388608 | tf_op jit(solution)/shard_map/section_backward/pallas_call | solution.py:171
  516.2 2.0 copy-done.29
  521.1 2.1 copy-done.30
  524.7 3.1 section_backward.20
  527.8 3.1 section_backward.21
  533.0 5.0 convert_bitcast_fusion.1
  538.0 5.0 convert_bitcast_fusion
  (206 shorter events, 88.9 us)
Async XLA Ops:
  59.9 8.2 %copy-start.72 = (s32[32]{0:T(128)S(1)}, s32[32]{0:T(128)}, u32[]{:S(2)}) copy-start(s32[32]{0:T(128)} %param.15) | copy-start | bytes 388
  59.9 63.1 %all-to-all-start.2 = ((bf16[32,64,1024]{2,1,0:T(8,128)(2,1)}), bf16[32,64,1024]{2,1,0:T(8,128)(2,1)}, u32[]{:S(2)}, u32[]{:S(2)}) async-start(bf16[32,64,1024]{2,1,0:T(8,128)(2,1)} %bitcast.97), calls=%async_computation.2 | async-start | bytes 8388608 | tf_op jit(solution)/shard_map/all_to_all | solution.py:229
  123.1 61.2 %all-to-all-start.1 = ((bf16[32,32,2048]{2,1,0:T(8,128)(2,1)}), bf16[32,32,2048]{2,1,0:T(8,128)(2,1)}, u32[]{:S(2)}, u32[]{:S(2)}) async-start(bf16[32,32,2048]{2,1,0:T(8,128)(2,1)} %gather_fusion), calls=%async_computation.1 | async-start | bytes 8388608 | tf_op jit(solution)/shard_map/all_to_all | solution.py:235
  135.1 57.7 %copy-start.75 = (s32[4]{0:T(128)S(1)}, s32[4]{0:T(128)}, u32[]{:S(2)}) copy-start(s32[4]{0:T(128)} %constant.67.clone) | copy-start | bytes 52
  135.1 59.4 %copy-start.73 = (s32[32]{0:T(128)S(1)}, s32[32]{0:T(128)}, u32[]{:S(2)}) copy-start(s32[32]{0:T(128)} %param.14) | copy-start | bytes 388
  184.3 64.1 %all-to-all-start.3 = ((bf16[32,64,1024]{2,1,0:T(8,128)(2,1)}), bf16[32,64,1024]{2,1,0:T(8,128)(2,1)}, u32[]{:S(2)}, u32[]{:S(2)}) async-start(bf16[32,64,1024]{2,1,0:T(8,128)(2,1)} %gather_fusion.1), calls=%async_computation.3 | async-start | bytes 8388608 | tf_op jit(solution)/shard_map/all_to_all | solution.py:235
  255.4 2.7 copy-start.69
  255.4 2.7 copy-start.71
  261.8 12.8 %collective-permute-start.1 = (bf16[192,1024]{1,0:T(8,128)(2,1)}, bf16[192,1024]{1,0:T(8,128)(2,1)}, u32[]{:S(2)}, u32[]{:S(2)}) collective-permute-start(bf16[192,1024]{1,0:T(8,128)(2,1)} %get-tuple-element.116), channel_id=1, source_target_pairs={{0,32},{1,33},{2,34},{3,35},{4,36},{5,37},{6,38},{7,39},{8,40},{9,... | collective-permute-start | bytes 1179656 | tf_op jit(solution)/shard_map/ppermute | solution.py:208
  266.9 2.0 copy-start.9
  271.5 21.3 %collective-permute-start = (bf16[192,1024]{1,0:T(8,128)(2,1)}, bf16[192,1024]{1,0:T(8,128)(2,1)}, u32[]{:S(2)}, u32[]{:S(2)}) collective-permute-start(bf16[192,1024]{1,0:T(8,128)(2,1)} %get-tuple-element.115), channel_id=1, source_target_pairs={{0,32},{1,33},{2,34},{3,35},{4,36},{5,37},{6,38},{7,39},{8,40},{9,... | collective-permute-start | bytes 1179656 | tf_op jit(solution)/shard_map/ppermute | solution.py:208
  274.7 2.1 copy-start.10
  287.7 40.1 %collective-permute-start.3 = (bf16[192,1024]{1,0:T(8,128)(2,1)}, bf16[192,1024]{1,0:T(8,128)(2,1)}, u32[]{:S(2)}, u32[]{:S(2)}) collective-permute-start(bf16[192,1024]{1,0:T(8,128)(2,1)} %get-tuple-element.128), channel_id=1, source_target_pairs={{32,64},{33,65},{34,66},{35,67},{36,68},{37,69},{38,70},{39,71},{4... | collective-permute-start | bytes 1179656 | tf_op jit(solution)/shard_map/ppermute | solution.py:208
  291.6 17.7 %collective-permute-start.4 = (bf16[192,1024]{1,0:T(8,128)(2,1)}, bf16[192,1024]{1,0:T(8,128)(2,1)}, u32[]{:S(2)}, u32[]{:S(2)}) collective-permute-start(bf16[192,1024]{1,0:T(8,128)(2,1)} %get-tuple-element.128), channel_id=1, source_target_pairs={{0,32},{1,33},{2,34},{3,35},{4,36},{5,37},{6,38},{7,39},{8,40},{9,... | collective-permute-start | bytes 1179656 | tf_op jit(solution)/shard_map/ppermute | solution.py:208
  300.7 2.0 copy-start.11
  305.3 22.4 %collective-permute-start.2 = (bf16[192,1024]{1,0:T(8,128)(2,1)}, bf16[192,1024]{1,0:T(8,128)(2,1)S(1)}, u32[]{:S(2)}, u32[]{:S(2)}) collective-permute-start(bf16[192,1024]{1,0:T(8,128)(2,1)} %get-tuple-element.127), channel_id=1, source_target_pairs={{0,32},{1,33},{2,34},{3,35},{4,36},{5,37},{6,38},{7,39},{8,40},{9,... | collective-permute-start | bytes 1179656 | tf_op jit(solution)/shard_map/ppermute | solution.py:208
  307.9 29.7 %collective-permute-start.6 = (bf16[192,1024]{1,0:T(8,128)(2,1)}, bf16[192,1024]{1,0:T(8,128)(2,1)S(1)}, u32[]{:S(2)}, u32[]{:S(2)}) collective-permute-start(bf16[192,1024]{1,0:T(8,128)(2,1)} %get-tuple-element.127), channel_id=1, source_target_pairs={{32,64},{33,65},{34,66},{35,67},{36,68},{37,69},{38,70},{39,71},{4... | collective-permute-start | bytes 1179656 | tf_op jit(solution)/shard_map/ppermute | solution.py:208
  309.3 2.1 copy-start
  311.4 2.1 copy-start.12
  324.3 2.0 copy-start.1
  326.3 25.6 %collective-permute-start.8 = (bf16[192,1024]{1,0:T(8,128)(2,1)}, bf16[192,1024]{1,0:T(8,128)(2,1)S(1)}, u32[]{:S(2)}, u32[]{:S(2)}) collective-permute-start(bf16[192,1024]{1,0:T(8,128)(2,1)} %get-tuple-element.146), channel_id=1, source_target_pairs={{32,64},{33,65},{34,66},{35,67},{36,68},{37,69},{38,70},{39,71},{4... | collective-permute-start | bytes 1179656 | tf_op jit(solution)/shard_map/ppermute | solution.py:208
  335.6 16.3 %collective-permute-start.9 = (bf16[192,1024]{1,0:T(8,128)(2,1)}, bf16[192,1024]{1,0:T(8,128)(2,1)S(1)}, u32[]{:S(2)}, u32[]{:S(2)}) collective-permute-start(bf16[192,1024]{1,0:T(8,128)(2,1)} %get-tuple-element.139), channel_id=1, source_target_pairs={{64,96},{65,97},{66,98},{67,99},{68,100},{69,101},{70,102},{71,103... | collective-permute-start | bytes 1179656 | tf_op jit(solution)/shard_map/ppermute | solution.py:208
  336.3 25.3 %collective-permute-start.5 = (bf16[192,1024]{1,0:T(8,128)(2,1)}, bf16[192,1024]{1,0:T(8,128)(2,1)S(1)}, u32[]{:S(2)}, u32[]{:S(2)}) collective-permute-start(bf16[192,1024]{1,0:T(8,128)(2,1)} %get-tuple-element.139), channel_id=1, source_target_pairs={{32,64},{33,65},{34,66},{35,67},{36,68},{37,69},{38,70},{39,71},{4... | collective-permute-start | bytes 1179656 | tf_op jit(solution)/shard_map/ppermute | solution.py:208
  337.6 2.1 copy-start.2
  349.4 12.2 %collective-permute-start.7 = (bf16[192,1024]{1,0:T(8,128)(2,1)}, bf16[192,1024]{1,0:T(8,128)(2,1)S(1)}, u32[]{:S(2)}, u32[]{:S(2)}) collective-permute-start(bf16[192,1024]{1,0:T(8,128)(2,1)} %get-tuple-element.145), channel_id=1, source_target_pairs={{64,96},{65,97},{66,98},{67,99},{68,100},{69,101},{70,102},{71,103... | collective-permute-start | bytes 1179656 | tf_op jit(solution)/shard_map/ppermute | solution.py:208
  351.9 2.1 copy-start.14
  360.9 12.7 %collective-permute-start.11 = (bf16[192,1024]{1,0:T(8,128)(2,1)}, bf16[192,1024]{1,0:T(8,128)(2,1)S(1)}, u32[]{:S(2)}, u32[]{:S(2)}) collective-permute-start(bf16[192,1024]{1,0:T(8,128)(2,1)} %get-tuple-element.158), channel_id=1, source_target_pairs={{64,96},{65,97},{66,98},{67,99},{68,100},{69,101},{70,102},{71,103... | collective-permute-start | bytes 1179656 | tf_op jit(solution)/shard_map/ppermute | solution.py:208
  361.6 9.6 %copy-start.74 = (s32[4]{0:T(128)S(1)}, s32[4]{0:T(128)}, u32[]{:S(2)}) copy-start(s32[4]{0:T(128)} %constant.68.clone) | copy-start | bytes 52
  369.9 14.1 %collective-permute-start.10 = (bf16[192,1024]{1,0:T(8,128)(2,1)S(1)}, bf16[192,1024]{1,0:T(8,128)(2,1)S(1)}, u32[]{:S(2)}, u32[]{:S(2)}) collective-permute-start(bf16[192,1024]{1,0:T(8,128)(2,1)S(1)} %get-tuple-element.157), channel_id=1, source_target_pairs={{64,96},{65,97},{66,98},{67,99},{68,100},{69,101},{70,102},{71,103... | collective-permute-start | bytes 1179656 | tf_op jit(solution)/shard_map/ppermute | solution.py:208
  373.6 2.1 copy-start.4
  375.7 2.1 copy-start.16
  390.3 2.5 copy-start.39
  390.6 2.6 copy-start.70
  396.2 12.4 %collective-permute-start.13 = (bf16[192,1024]{1,0:T(8,128)(2,1)}, bf16[192,1024]{1,0:T(8,128)(2,1)}, u32[]{:S(2)}, u32[]{:S(2)}) collective-permute-start(bf16[192,1024]{1,0:T(8,128)(2,1)} %get-tuple-element.176), channel_id=1, source_target_pairs={{96,64},{97,65},{98,66},{99,67},{100,68},{101,69},{102,70},{103,71... | collective-permute-start | bytes 1179656 | tf_op jit(solution)/shard_map/ppermute | solution.py:208
  400.7 2.0 copy-start.19
  405.3 14.7 %collective-permute-start.12 = (bf16[192,1024]{1,0:T(8,128)(2,1)}, bf16[192,1024]{1,0:T(8,128)(2,1)}, u32[]{:S(2)}, u32[]{:S(2)}) collective-permute-start(bf16[192,1024]{1,0:T(8,128)(2,1)} %get-tuple-element.175), channel_id=1, source_target_pairs={{96,64},{97,65},{98,66},{99,67},{100,68},{101,69},{102,70},{103,71... | collective-permute-start | bytes 1179656 | tf_op jit(solution)/shard_map/ppermute | solution.py:208
  408.7 2.1 copy-start.20
  417.1 28.5 %collective-permute-start.15 = (bf16[192,1024]{1,0:T(8,128)(2,1)}, bf16[192,1024]{1,0:T(8,128)(2,1)}, u32[]{:S(2)}, u32[]{:S(2)}) collective-permute-start(bf16[192,1024]{1,0:T(8,128)(2,1)} %get-tuple-element.184), channel_id=1, source_target_pairs={{64,32},{65,33},{66,34},{67,35},{68,36},{69,37},{70,38},{71,39},{7... | collective-permute-start | bytes 1179656 | tf_op jit(solution)/shard_map/ppermute | solution.py:208
  418.4 13.4 %collective-permute-start.17 = (bf16[192,1024]{1,0:T(8,128)(2,1)}, bf16[192,1024]{1,0:T(8,128)(2,1)}, u32[]{:S(2)}, u32[]{:S(2)}) collective-permute-start(bf16[192,1024]{1,0:T(8,128)(2,1)} %get-tuple-element.184), channel_id=1, source_target_pairs={{96,64},{97,65},{98,66},{99,67},{100,68},{101,69},{102,70},{103,71... | collective-permute-start | bytes 1179656 | tf_op jit(solution)/shard_map/ppermute | solution.py:208
  423.3 2.0 copy-start.21
  427.9 17.7 %collective-permute-start.16 = (bf16[192,1024]{1,0:T(8,128)(2,1)}, bf16[192,1024]{1,0:T(8,128)(2,1)S(1)}, u32[]{:S(2)}, u32[]{:S(2)}) collective-permute-start(bf16[192,1024]{1,0:T(8,128)(2,1)} %get-tuple-element.183), channel_id=1, source_target_pairs={{96,64},{97,65},{98,66},{99,67},{100,68},{101,69},{102,70},{103,71... | collective-permute-start | bytes 1179656 | tf_op jit(solution)/shard_map/ppermute | solution.py:208
  430.4 33.5 %collective-permute-start.14 = (bf16[192,1024]{1,0:T(8,128)(2,1)}, bf16[192,1024]{1,0:T(8,128)(2,1)S(1)}, u32[]{:S(2)}, u32[]{:S(2)}) collective-permute-start(bf16[192,1024]{1,0:T(8,128)(2,1)} %get-tuple-element.183), channel_id=1, source_target_pairs={{64,32},{65,33},{66,34},{67,35},{68,36},{69,37},{70,38},{71,39},{7... | collective-permute-start | bytes 1179656 | tf_op jit(solution)/shard_map/ppermute | solution.py:208
  431.7 2.1 copy-start.6
  433.9 2.1 copy-start.22
  442.3 2.0 copy-start.23
  445.6 2.1 copy-start.24
  449.3 14.6 %copy-start.7 = (bf16[960,2048]{1,0:T(8,128)(2,1)S(1)}, bf16[960,2048]{1,0:T(8,128)(2,1)}, u32[]{:S(2)}) copy-start(bf16[960,2048]{1,0:T(8,128)(2,1)} %copy-done.5) | copy-start | bytes 11796484
  458.0 2.0 copy-start.25
  460.0 47.0 %collective-permute-start.19 = (bf16[192,1024]{1,0:T(8,128)(2,1)}, bf16[192,1024]{1,0:T(8,128)(2,1)S(1)}, u32[]{:S(2)}, u32[]{:S(2)}) collective-permute-start(bf16[192,1024]{1,0:T(8,128)(2,1)} %get-tuple-element.195), channel_id=1, source_target_pairs={{64,32},{65,33},{66,34},{67,35},{68,36},{69,37},{70,38},{71,39},{7... | collective-permute-start | bytes 1179656 | tf_op jit(solution)/shard_map/ppermute | solution.py:208
  461.3 20.0 %collective-permute-start.20 = (bf16[192,1024]{1,0:T(8,128)(2,1)}, bf16[192,1024]{1,0:T(8,128)(2,1)S(1)}, u32[]{:S(2)}, u32[]{:S(2)}) collective-permute-start(bf16[192,1024]{1,0:T(8,128)(2,1)} %get-tuple-element.195), channel_id=1, source_target_pairs={{32,0},{33,1},{34,2},{35,3},{36,4},{37,5},{38,6},{39,7},{40,8},{41... | collective-permute-start | bytes 1179656 | tf_op jit(solution)/shard_map/ppermute | solution.py:208
  462.6 29.3 %collective-permute-start.21 = (bf16[192,1024]{1,0:T(8,128)(2,1)}, bf16[192,1024]{1,0:T(8,128)(2,1)S(1)}, u32[]{:S(2)}, u32[]{:S(2)}) collective-permute-start(bf16[192,1024]{1,0:T(8,128)(2,1)} %get-tuple-element.196), channel_id=1, source_target_pairs={{64,32},{65,33},{66,34},{67,35},{68,36},{69,37},{70,38},{71,39},{7... | collective-permute-start | bytes 1179656 | tf_op jit(solution)/shard_map/ppermute | solution.py:208
  463.9 2.1 copy-start.26
  474.0 2.0 copy-start.27
  478.6 28.4 %collective-permute-start.18 = (bf16[192,1024]{1,0:T(8,128)(2,1)}, bf16[192,1024]{1,0:T(8,128)(2,1)S(1)}, u32[]{:S(2)}, u32[]{:S(2)}) collective-permute-start(bf16[192,1024]{1,0:T(8,128)(2,1)} %get-tuple-element.194), channel_id=1, source_target_pairs={{32,0},{33,1},{34,2},{35,3},{36,4},{37,5},{38,6},{39,7},{40,8},{41... | collective-permute-start | bytes 1179656 | tf_op jit(solution)/shard_map/ppermute | solution.py:208
  491.9 2.1 copy-start.28
  505.7 15.4 %collective-permute-start.23 = (bf16[192,1024]{1,0:T(8,128)(2,1)S(1)}, bf16[192,1024]{1,0:T(8,128)(2,1)S(1)}, u32[]{:S(2)}, u32[]{:S(2)}) collective-permute-start(bf16[192,1024]{1,0:T(8,128)(2,1)S(1)} %get-tuple-element.204), channel_id=1, source_target_pairs={{32,0},{33,1},{34,2},{35,3},{36,4},{37,5},{38,6},{39,7},{40,8},{41... | collective-permute-start | bytes 1179656 | tf_op jit(solution)/shard_map/ppermute | solution.py:208
  508.6 11.2 %copy-start.40 = (bf16[960,1024]{1,0:T(8,128)(2,1)S(1)}, bf16[960,1024]{1,0:T(8,128)(2,1)}, u32[]{:S(2)}) copy-start(bf16[960,1024]{1,0:T(8,128)(2,1)} %copy-done.39) | copy-start | bytes 5898244
  508.6 12.5 %copy-start.8 = (bf16[960,2048]{1,0:T(8,128)(2,1)S(1)}, bf16[960,2048]{1,0:T(8,128)(2,1)}, u32[]{:S(2)}) copy-start(bf16[960,2048]{1,0:T(8,128)(2,1)} %copy-done.5) | copy-start | bytes 11796484
  516.2 2.0 copy-start.29
  518.2 2.8 copy-start.49
  518.2 9.6 %collective-permute-start.22 = (bf16[192,1024]{1,0:T(8,128)(2,1)S(1)}, bf16[192,1024]{1,0:T(8,128)(2,1)S(1)}, u32[]{:S(2)}, u32[]{:S(2)}) collective-permute-start(bf16[192,1024]{1,0:T(8,128)(2,1)S(1)} %get-tuple-element.203), channel_id=1, source_target_pairs={{32,0},{33,1},{34,2},{35,3},{36,4},{37,5},{38,6},{39,7},{40,8},{41... | collective-permute-start | bytes 1179656 | tf_op jit(solution)/shard_map/ppermute | solution.py:208
  521.1 2.1 copy-start.30
  530.8 2.1 copy-start.60
  533.0 5.0 copy-start.18
  (39 other events, 58.3 us)

commit v2 on v1

v2 whole, which is shorter than its diff:
```python
import functools

import jax
import jax.numpy as jnp
from jax import lax
from jax.experimental import pallas as pl
from jax.experimental.pallas import tpu as pltpu
from jax.sharding import PartitionSpec as P

MICRO = 4
CHUNK = 512
LAG_FAST = 2
LAG_SLOW = 3
GELU_C = 0.7978845608028654
VMEM_LIMIT = 24 * 1024 * 1024


def row_stats(values):
    center = values - jnp.mean(values, axis=-1, keepdims=True)
    factor = lax.rsqrt(jnp.mean(center * center, axis=-1, keepdims=True) + 1e-05)
    return center * factor, factor


def mm(left, right, left_dim, right_dim):
    return lax.dot_general(
        left, right, (((left_dim,), (right_dim,)), ((), ())), preferred_element_type=jnp.float32
    )


def choose(level, sources):
    value = sources[-1][1][...]
    for levels, ref in sources[:-1]:
        hit = functools.reduce(jnp.logical_or, [level == k for k in levels])
        value = jnp.where(hit, ref[...], value)
    return value


def forward_body(levels_of, n_stash, meta, *refs):
    n_src = len(levels_of)
    sources = list(zip(levels_of, refs[:n_src]))
    gain, up, down = refs[n_src : n_src + 3]
    refs = refs[n_src + 3 + n_stash :]
    send, rows_h, normed_h, hidden_h, slope_h, out_h = refs[:6]
    rows_s, normed_s, hidden_s, slope_s, sems = refs[6:]
    m, hidden_width = hidden_s.shape
    place = pl.ds(pl.multiple_of(meta[0] * m, m), m)

    def store(k, source, target):
        return pltpu.make_async_copy(source, target.at[place, :], sems.at[k])

    @pl.when(meta[1] == 1)
    def _():
        rows = choose(meta[2], sources)
        rows_s[...] = rows
        xhat, _ = row_stats(rows.astype(jnp.float32))
        normed_s[...] = (xhat * gain[...]).astype(jnp.bfloat16)
        store(0, rows_s, rows_h).start()
        store(1, normed_s, normed_h).start()
        for j in range(hidden_width // CHUNK):
            cut = slice(j * CHUNK, (j + 1) * CHUNK)
            u = mm(normed_s[...], up[:, cut], 1, 0)
            inner = jnp.tanh(GELU_C * (u + 0.044715 * u * u * u))
            half = 0.5 * (1.0 + inner)
            hidden_s[:, cut] = (u * half).astype(jnp.bfloat16)
            slope_s[:, cut] = (
                half + 0.5 * u * (1.0 - inner * inner) * GELU_C * (1.0 + 3.0 * 0.044715 * u * u)
            ).astype(jnp.bfloat16)
        store(2, hidden_s, hidden_h).start()
        store(3, slope_s, slope_h).start()
        total = rows_s[...].astype(jnp.float32) + mm(hidden_s[...], down[...], 1, 0)
        send[...] = total.astype(jnp.bfloat16)
        store(4, send, out_h).start()
        for k, (source, target) in enumerate(
            [(rows_s, rows_h), (normed_s, normed_h), (hidden_s, hidden_h), (slope_s, slope_h), (send, out_h)]
        ):
            store(k, source, target).wait()


def backward_body(levels_of, n_stash, meta, *refs):
    n_src = len(levels_of)
    sources = list(zip(levels_of, refs[:n_src]))
    gain, up, down, rows_h, slope_h = refs[n_src : n_src + 5]
    refs = refs[n_src + 5 + n_stash :]
    send, grad_h, pre_h, grad_in_h = refs[:4]
    grad_s, rows_s, slope_s, pre_s, sems = refs[4:]
    m, hidden_width = pre_s.shape
    place = pl.ds(pl.multiple_of(meta[0] * m, m), m)

    def store(k, source, target):
        return pltpu.make_async_copy(source, target.at[place, :], sems.at[k])

    def load(k, source, target):
        return pltpu.make_async_copy(source.at[place, :], target, sems.at[k])

    @pl.when(meta[1] == 1)
    def _():
        load(0, slope_h, slope_s).start()
        load(1, rows_h, rows_s).start()
        grad_s[...] = choose(meta[2], sources)
        store(2, grad_s, grad_h).start()
        load(0, slope_h, slope_s).wait()
        for j in range(hidden_width // CHUNK):
            cut = slice(j * CHUNK, (j + 1) * CHUNK)
            grad_hidden = mm(grad_s[...], down[cut, :], 1, 1)
            pre_s[:, cut] = (grad_hidden * slope_s[:, cut].astype(jnp.float32)).astype(jnp.bfloat16)
        store(3, pre_s, pre_h).start()
        load(1, rows_h, rows_s).wait()
        q = mm(pre_s[...], up[...], 1, 1) * gain[...]
        xhat, factor = row_stats(rows_s[...].astype(jnp.float32))
        centered = (
            q
            - jnp.mean(q, axis=-1, keepdims=True)
            - xhat * jnp.mean(q * xhat, axis=-1, keepdims=True)
        )
        send[...] = (grad_s[...].astype(jnp.float32) + factor * centered).astype(jnp.bfloat16)
        store(4, send, grad_in_h).start()
        store(2, grad_s, grad_h).wait()
        store(3, pre_s, pre_h).wait()
        store(4, send, grad_in_h).wait()


def stage(body, name, meta, sources, weights, reads, stash, shapes, m, flops, scratch):
    gain, up, down = weights
    width, hidden = up.shape
    whole = pl.BlockSpec(memory_space=pltpu.VMEM)
    far = pl.BlockSpec(memory_space=pltpu.HBM)
    in_specs = []
    for _, kind, _ in sources:
        if kind == "slot":
            in_specs.append(
                pl.BlockSpec((m, width), lambda j, meta: (jnp.minimum(meta[0], MICRO - 1), 0))
            )
        else:
            in_specs.append(pl.BlockSpec((m, width), lambda j, meta: (0, 0)))
    in_specs += [whole] * 3 + [far] * len(reads)
    n_before = len(in_specs)
    held = stash or []
    in_specs += [far] * len(held)
    out_specs = [pl.BlockSpec((m, width), lambda j, meta: (0, 0))] + [far] * len(shapes)
    outs = [jax.ShapeDtypeStruct((m, width), jnp.bfloat16)]
    outs += [jax.ShapeDtypeStruct(s, jnp.bfloat16) for s in shapes]
    call = pl.pallas_call(
        functools.partial(body, [levels for levels, _, _ in sources], len(held)),
        grid_spec=pltpu.PrefetchScalarGridSpec(
            num_scalar_prefetch=1,
            grid=(1,),
            in_specs=in_specs,
            out_specs=out_specs,
            scratch_shapes=scratch + [pltpu.SemaphoreType.DMA((5,))],
        ),
        out_shape=outs,
        input_output_aliases={1 + n_before + i: 1 + i for i in range(len(held))},
        compiler_params=pltpu.CompilerParams(
            dimension_semantics=("arbitrary",), vmem_limit_bytes=VMEM_LIMIT
        ),
        cost_estimate=pl.CostEstimate(
            flops=flops, bytes_accessed=2 * 2 * width * hidden, transcendentals=0
        ),
        name=name,
    )
    result = call(meta, *[a for _, _, a in sources], gain, up, down, *reads, *held)
    return result[0], list(result[1:])


def relay(body, name, entry, offsets, direction, level, weights, reads, columns, m, scratch):
    depth = len(offsets)
    width, hidden = weights[1].shape
    flops = 4 * m * width * hidden
    shapes = [(MICRO * m, c) for c in columns]
    rounds = max(offsets) + MICRO
    head = 0 if direction > 0 else depth - 1
    offset = jnp.asarray(offsets, jnp.int32)[level]
    arrays = {}
    stash = None
    for turn in range(rounds):
        active = [s for s in range(depth) if 0 <= turn - offsets[s] < MICRO]
        index = turn - offset
        valid = (index >= 0) & (index < MICRO)
        slot = jnp.clip(index, 0, MICRO - 1)
        meta = jnp.stack([slot, valid.astype(jnp.int32), level]).astype(jnp.int32)
        by_array = {}
        for s in active:
            lag = None if s == head else offsets[s] - offsets[s - direction]
            by_array.setdefault(lag, []).append(s)
        sources = [
            (levels, "slot", entry) if lag is None else (levels, "whole", arrays[turn - lag, lag])
            for lag, levels in by_array.items()
        ]
        send, stash = stage(body, name, meta, sources, weights, reads, stash, shapes, m, flops, scratch)
        groups = {}
        for s in active:
            if 0 <= s + direction < depth:
                groups.setdefault(offsets[s + direction] - offsets[s], []).append(s)
        for lag, members in groups.items():
            arrays[turn, lag] = lax.ppermute(send, "section", [(s, s + direction) for s in members])
    return stash


def per_device(x_in, cotangent, norm_gain, w_up, w_down, live, donor):
    member = lax.axis_index("rep")
    level = lax.axis_index("section")
    depth = lax.axis_size("section")
    peers = lax.axis_size("rep")
    own_up = w_up[0, 0]
    own_down = w_down[0, 0]
    width, hidden_width = own_up.shape
    tokens = x_in.shape[1]
    m = tokens // MICRO

    def spread(own):
        return lax.all_to_all(
            own.reshape(peers, -1, own.shape[1]), "rep", split_axis=0, concat_axis=0, tiled=True
        )

    def collect(pieces):
        picked = pieces.at[donor].get(mode="promise_in_bounds")
        back = lax.all_to_all(picked, "rep", split_axis=0, concat_axis=0, tiled=True)
        return back.reshape(-1, back.shape[-1])

    alive = live[member] == 1
    held_up = spread(own_up)
    held_down = spread(own_down)
    used_up = jnp.where(alive, own_up, collect(held_up))
    used_down = jnp.where(alive, own_down, collect(held_down))
    weights = (norm_gain, used_up, used_down)
    lags = [LAG_SLOW if s % 2 else LAG_FAST for s in range(depth - 1)]
    offsets = [sum(lags[:s]) for s in range(depth)]

    def rows_of(columns):
        return pltpu.VMEM((m, columns), jnp.bfloat16)

    rows, normed, hidden, slope, outs = relay(
        forward_body, "section_forward", x_in[0], offsets, 1, level, weights, [],
        [width, width, hidden_width, hidden_width, width], m,
        [rows_of(width), rows_of(width), rows_of(hidden_width), rows_of(hidden_width)],
    )
    grads, pres, grads_in = relay(
        backward_body, "section_backward", cotangent[0], offsets[::-1], -1, level, weights,
        [rows, slope], [width, hidden_width, width], m,
        [rows_of(width), rows_of(width), rows_of(hidden_width), rows_of(hidden_width)],
    )
    grad_up = mm(normed, pres, 0, 0).astype(jnp.bfloat16)
    grad_down = mm(hidden, grads, 0, 0).astype(jnp.bfloat16)
    return (outs[None, None], grads_in[None, None], grad_up[None, None], grad_down[None, None])


def solution(mesh):
    return jax.shard_map(
        per_device,
        mesh=mesh,
        in_specs=(
            P("rep", None, None),
            P("rep", None, None),
            P("section", None),
            P("rep", "section", None, None),
            P("rep", "section", None, None),
            P(),
            P(),
        ),
        out_specs=(
            P("rep", "section", None, None),
            P("rep", "section", None, None),
            P("rep", "section", None, None),
            P("rep", "section", None, None),
        ),
        check_vma=False,
    )
```

time: 554 us -> 404 us (0.73)
  the two profiles are of different devices: /device:TPU:5 before, /device:TPU:64 now
where the time goes in v2:
time: 404 us; the launch traced here: 396 us
  waiting for transfers between devices  189 us (47%)
  blocking collectives  60.6 us (15%)
  Pallas kernels  54.1 us (13%)
  starting transfers between devices  41.3 us (10%)
  between operations  16.8 us (4%)
  local copies, waits for them, and re-layouts  12.5 us (3%)
  other arithmetic  11.5 us (3%)
  matrix products  10.2 us (3%)
    all_to_all x2, waiting for transfers between devices, collect(): lax.all_to_all(picked, 'rep', split_axis=0, concat_axis=0, tiled=True)  99.1 us
    all_to_all x1, blocking collectives, spread(): lax.all_to_all(own.reshape(peers, -1, own.shape[1]), 'rep', split_axis=0,...  60.6 us
    pallas_call x22, Pallas kernels, stage(): call(meta, *[a for _, _, a in sources], gain, up, down, *reads, *held)  54.1 us
    all_to_all x1, waiting for transfers between devices, spread(): lax.all_to_all(own.reshape(peers, -1, own.shape[1]), 'rep', split_axis=0,...  51 us
    ppermute x24, waiting for transfers between devices, relay(): lax.ppermute(send, 'section', [(s, s + direction) for s in members])  38.7 us
    ppermute x24, starting transfers between devices, relay(): lax.ppermute(send, 'section', [(s, s + direction) for s in members])  21.6 us
    all_to_all x2, starting transfers between devices, collect(): lax.all_to_all(picked, 'rep', split_axis=0, concat_axis=0, tiled=True)  12.9 us
    dot_general x2, matrix products, mm(): lax.dot_general(left, right, (((left_dim,), (right_dim,)), ((), ())), pre...  10.2 us
  transfers between devices with their start and end apart: 27, of which 7 were waited for; matrix products, arithmetic and copies ran while one was open for 5% of the time, Pallas kernels for 10%

profile of v2, /device:TPU:64, one launch (start us, length us, event | category | flops | bytes accessed | tf_op | source)
XLA Modules:
  0.0 395.6 jit_solution(1838401271967538355)
XLA Ops:
  0.6 60.6 %all_to_all.20 = bf16[32,64,1024]{2,1,0:T(8,128)(2,1)} all-to-all(bf16[32,64,1024]{2,1,0:T(8,128)(2,1)} %bitcast.34), channel_id=1, replica_groups=mesh['section'=4,'rep'=32] {'rep'}, dimensions={0} | all-to-all | bytes 8388608 | tf_op jit(solution)/shard_map/all_to_all | solution.py:211
  61.2 6.8 %all-to-all-start = ((bf16[32,32,2048]{2,1,0:T(8,128)(2,1)}), bf16[32,32,2048]{2,1,0:T(8,128)(2,1)}, u32[]{:S(2)}, u32[]{:S(2)}) async-start(bf16[32,32,2048]{2,1,0:T(8,128)(2,1)} %bitcast.35), calls=%async_computation | async-start | bytes 8388608 | tf_op jit(solution)/shard_map/all_to_all | solution.py:211
  68.0 5.0 %gather_fusion.1 = bf16[32,64,1024]{2,1,0:T(8,128)(2,1)} fusion(bf16[32,64,1024]{2,1,0:T(8,128)(2,1)} %all_to_all.20, s32[1024]{0:T(1024)S(1)} %pad_clamp_fusion), kind=kCustom, calls=%fused_computation.1 | custom fusion | bytes 8388736 | tf_op jit(solution)/shard_map/gather | solution.py:216
  73.0 51.0 %all-to-all-done = bf16[32,32,2048]{2,1,0:T(8,128)(2,1)} async-done(((bf16[32,32,2048]{2,1,0:T(8,128)(2,1)}), bf16[32,32,2048]{2,1,0:T(8,128)(2,1)}, u32[]{:S(2)}, u32[]{:S(2)}) %all-to-all-start) | async-done | bytes 4194336 | tf_op jit(solution)/shard_map/all_to_all | solution.py:211
  124.0 6.3 %all-to-all-start.3 = ((bf16[32,64,1024]{2,1,0:T(8,128)(2,1)}), bf16[32,64,1024]{2,1,0:T(8,128)(2,1)}, u32[]{:S(2)}, u32[]{:S(2)}) async-start(bf16[32,64,1024]{2,1,0:T(8,128)(2,1)} %gather_fusion.1), calls=%async_computation.3 | async-start | bytes 8388608 | tf_op jit(solution)/shard_map/all_to_all | solution.py:217
  130.3 5.0 %gather_fusion = bf16[32,32,2048]{2,1,0:T(8,128)(2,1)} fusion(bf16[32,32,2048]{2,1,0:T(8,128)(2,1)} %all-to-all-done, s32[1024]{0:T(1024)S(1)} %pad_clamp_fusion), kind=kCustom, calls=%fused_computation | custom fusion | bytes 8388736 | tf_op jit(solution)/shard_map/gather | solution.py:216
  135.3 50.3 %all-to-all-done.3 = bf16[32,64,1024]{2,1,0:T(8,128)(2,1)} async-done(((bf16[32,64,1024]{2,1,0:T(8,128)(2,1)}), bf16[32,64,1024]{2,1,0:T(8,128)(2,1)}, u32[]{:S(2)}, u32[]{:S(2)}) %all-to-all-start.3) | async-done | bytes 4194336 | tf_op jit(solution)/shard_map/all_to_all | solution.py:217
  185.6 6.7 %all-to-all-start.1 = ((bf16[32,32,2048]{2,1,0:T(8,128)(2,1)}), bf16[32,32,2048]{2,1,0:T(8,128)(2,1)}, u32[]{:S(2)}, u32[]{:S(2)}) async-start(bf16[32,32,2048]{2,1,0:T(8,128)(2,1)} %gather_fusion), calls=%async_computation.1 | async-start | bytes 8388608 | tf_op jit(solution)/shard_map/all_to_all | solution.py:217
  195.6 5.9 %bitcast_select_fusion.refs_3_.refs_4_ = bf16[2048,1024]{1,0:T(8,128)(2,1)} fusion(bf16[32,64,1024]{2,1,0:T(8,128)(2,1)} %all-to-all-done.3, bf16[1,1,2048,1024]{3,2,1,0:T(8,128)(2,1)} %param.13, pred[]{:T(512)} %bitcast.2), kind=kLoop, calls=%fused_computation.2 | loop fusion | flops 2097152 | bytes 12582913 | tf_op jit(solution)/shard_map/jit(_where)/select_n | solution.py:224
  201.5 48.7 %all-to-all-done.1 = bf16[32,32,2048]{2,1,0:T(8,128)(2,1)} async-done(((bf16[32,32,2048]{2,1,0:T(8,128)(2,1)}), bf16[32,32,2048]{2,1,0:T(8,128)(2,1)}, u32[]{:S(2)}, u32[]{:S(2)}) %all-to-all-start.1) | async-done | bytes 4194336 | tf_op jit(solution)/shard_map/all_to_all | solution.py:217
  250.2 4.0 %bitcast_select_fusion.1.refs_2_.refs_3_ = bf16[1024,2048]{1,0:T(8,128)(2,1)S(1)} fusion(bf16[32,32,2048]{2,1,0:T(8,128)(2,1)} %all-to-all-done.1, bf16[1,1,1024,2048]{3,2,1,0:T(8,128)(2,1)} %param.12, pred[]{:T(512)} %bitcast.2), kind=kLoop, calls=%fused_computation.3 | loop fusion | flops 2097152 | bytes 12582913 | tf_op jit(solution)/shard_map/jit(_where)/select_n | solution.py:223
  254.9 5.0 %section_forward.11 = (bf16[192,1024]{1,0:T(8,128)(2,1)S(1)}, bf16[768,1024]{1,0:T(8,128)(2,1)S(1)}, bf16[768,1024]{1,0:T(8,128)(2,1)S(1)}, bf16[768,2048]{1,0:T...) custom-call(s32[3]{0:T(128)S(1)} %get-tuple-element.217.meta, bf16[768,1024]{1,0:T(8,128)(2,1)S(1)} %bitcast.24, ...), custom_call_target="tpu_custom_call" | custom-call | flops 1610612736 | bytes 8388608 | tf_op jit(solution)/shard_map/section_forward/pallas_call | solution.py:161
  259.9 1.3 collective-permute-start.1
  261.2 5.1 %section_forward.12 = (bf16[192,1024]{1,0:T(8,128)(2,1)S(1)}, bf16[768,1024]{1,0:T(8,128)(2,1)S(1)}, bf16[768,1024]{1,0:T(8,128)(2,1)S(1)}, bf16[768,2048]{1,0:T...) custom-call(s32[3]{0:T(128)S(1)} %get-tuple-element.216.meta, ...), custom_call_target="tpu_custom_call", output_to_operand_aliasing={{1}: (5, {}), {2}: (6, {}), {3}: (7, {}), {4}: (8, {}), {5}... | custom-call | flops 1610612736 | bytes 8388608 | tf_op jit(solution)/shard_map/section_forward/pallas_call | solution.py:161
  266.3 1.3 collective-permute-start
  269.7 5.2 %section_forward.13 = (bf16[192,1024]{1,0:T(8,128)(2,1)S(1)}, bf16[768,1024]{1,0:T(8,128)(2,1)S(1)}, bf16[768,1024]{1,0:T(8,128)(2,1)S(1)}, bf16[768,2048]{1,0:T...) custom-call(s32[3]{0:T(128)S(1)} %add_add_fusion.6.meta, ...), custom_call_target="tpu_custom_call", output_to_operand_aliasing={{1}: (6, {}), {2}: (7, {}), {3}: (8, {}), {4}: (9, {}), {5}... | custom-call | flops 1610612736 | bytes 8388608 | tf_op jit(solution)/shard_map/section_forward/pallas_call | solution.py:161
  274.9 1.3 collective-permute-start.4
  276.3 0.7 collective-permute-start.3
  277.0 5.0 %section_forward.14 = (bf16[192,1024]{1,0:T(8,128)(2,1)S(1)}, bf16[768,1024]{1,0:T(8,128)(2,1)S(1)}, bf16[768,1024]{1,0:T(8,128)(2,1)S(1)}, bf16[768,2048]{1,0:T...) custom-call(s32[3]{0:T(128)S(1)} %add_add_fusion.3.meta, ...), custom_call_target="tpu_custom_call", output_to_operand_aliasing={{1}: (6, {}), {2}: (7, {}), {3}: (8, {}), {4}: (9, {}), {5}... | custom-call | flops 1610612736 | bytes 8388608 | tf_op jit(solution)/shard_map/section_forward/pallas_call | solution.py:161
  282.0 1.3 collective-permute-start.2
  284.8 0.7 collective-permute-start.6
  285.6 0.6 section_forward.15
  286.2 0.6 section_forward.16
  286.8 0.7 collective-permute-start.9
  287.5 0.9 collective-permute-start.8
  288.4 0.6 section_forward.17
  289.0 0.7 collective-permute-start.7
  289.7 0.7 collective-permute-start.5
  292.5 0.6 section_forward.18
  293.2 0.7 collective-permute-start.11
  293.9 0.6 section_forward.19
  294.5 0.7 collective-permute-start.10
  295.9 0.6 dynamic_slice.11
  298.0 1.7 section_forward.20
  299.8 1.3 section_forward.21
  301.2 0.6 section_backward.11
  301.8 0.7 collective-permute-start.13
  302.5 0.6 section_backward.12
  303.1 0.7 collective-permute-start.12
  305.2 1.4 section_backward.13
  306.7 0.7 collective-permute-start.17
  307.4 0.6 section_backward.14
  308.0 0.7 collective-permute-start.16
  308.7 0.7 collective-permute-start.15
  311.5 0.7 collective-permute-start.14
  312.2 0.6 section_backward.15
  312.8 0.6 section_backward.16
  313.4 1.3 collective-permute-start.20
  314.7 0.7 collective-permute-start.21
  315.5 0.8 section_backward.17
  316.3 1.3 collective-permute-start.18
  317.6 0.7 collective-permute-start.19
  319.8 35.1 %collective-permute-done.20.refs_0_ = bf16[192,1024]{1,0:T(8,128)(2,1)S(1)} collective-permute-done((bf16[192,1024]{1,0:T(8,128)(2,1)S(1)}, bf16[192,1024]{1,0:T(8,128)(2,1)S(1)}, u32[]{:S(2)}, u32[]{:S(2)}) %collective-permute-start.20) | collective-permute-done | bytes 393248 | tf_op jit(solution)/shard_map/ppermute | solution.py:195
  354.9 5.2 %section_backward.18 = (bf16[192,1024]{1,0:T(8,128)(2,1)S(1)}, bf16[768,1024]{1,0:T(8,128)(2,1)S(1)}, bf16[768,2048]{1,0:T(8,128)(2,1)S(1)}, bf16[768,1024]{1,0:T(8,128)(2,1)}) custom-call(s32[3]{0:T(128)S(1)} %add_add_fusion.20.meta, ...), custom_call_target="tpu_custom_call", output_to_operand_aliasing={{1}: (8, {}), {2}: (9, {}), {3}: (10, {})} | custom-call | flops 1610612736 | bytes 8388608 | tf_op jit(solution)/shard_map/section_backward/pallas_call | solution.py:161
  360.0 1.3 collective-permute-start.23
  361.3 1.6 collective-permute-done.18.refs_0_
  363.0 5.2 %section_backward.19 = (bf16[192,1024]{1,0:T(8,128)(2,1)S(1)}, bf16[768,1024]{1,0:T(8,128)(2,1)S(1)}, bf16[768,2048]{1,0:T(8,128)(2,1)S(1)}, bf16[768,1024]{1,0:T(8,128)(2,1)}) custom-call(s32[3]{0:T(128)S(1)} %add_add_fusion.12.meta, ...), custom_call_target="tpu_custom_call", output_to_operand_aliasing={{1}: (8, {}), {2}: (9, {}), {3}: (10, {})} | custom-call | flops 1610612736 | bytes 8388608 | tf_op jit(solution)/shard_map/section_backward/pallas_call | solution.py:161
  368.1 1.3 collective-permute-start.22
  370.9 1.3 collective-permute-done.23.refs_0_
  372.2 5.9 %section_backward.20 = (bf16[192,1024]{1,0:T(8,128)(2,1)}, bf16[768,1024]{1,0:T(8,128)(2,1)S(1)}, bf16[768,2048]{1,0:T(8,128)(2,1)S(1)}, bf16[768,1024]{1,0:T(8,128)(2,1)}) custom-call(s32[3]{0:T(128)S(1)} %add_add_fusion.21.meta, bf16[192,1024]{1,0:T(8,128)(2,1)S(1)} %collective-permute-done.23.refs_0_, ...), custom_call_target="tpu_custom_call", output_to_operand_aliasing={{1}: (7, {}), {2}: (8, {}), {3}: (9, {})} | custom-call | flops 1610612736 | bytes 8388608 | tf_op jit(solution)/shard_map/section_backward/pallas_call | solution.py:161
  378.2 0.6 collective-permute-done.22.refs_0_
  378.8 6.2 %section_backward.21 = (bf16[192,1024]{1,0:T(8,128)(2,1)}, bf16[768,1024]{1,0:T(8,128)(2,1)S(1)}, bf16[768,2048]{1,0:T(8,128)(2,1)S(1)}, bf16[768,1024]{1,0:T(8,128)(2,1)}) custom-call(s32[3]{0:T(128)S(1)} %add_add_fusion.11.meta, bf16[192,1024]{1,0:T(8,128)(2,1)S(1)} %collective-permute-done.22.refs_0_, ...), custom_call_target="tpu_custom_call", output_to_operand_aliasing={{1}: (7, {}), {2}: (8, {}), {3}: (9, {})} | custom-call | flops 1610612736 | bytes 8388608 | tf_op jit(solution)/shard_map/section_backward/pallas_call | solution.py:161
  385.0 5.1 %convert_bitcast_fusion = bf16[1,1,2048,1024]{3,2,1,0:T(8,128)(2,1)} fusion(bf16[768,2048]{1,0:T(8,128)(2,1)S(1)} %get-tuple-element.214, bf16[768,1024]{1,0:T(8,128)(2,1)S(1)} %get-tuple-element.215), kind=kOutput, calls=%fused_computation.4 | convolution fusion | flops 3223322624 | bytes 8912896 | tf_op jit(solution)/shard_map/dot_general | solution.py:25
  390.1 5.0 %convert_bitcast_fusion.1 = bf16[1,1,1024,2048]{3,2,1,0:T(8,128)(2,1)} fusion(bf16[768,1024]{1,0:T(8,128)(2,1)S(1)} %get-tuple-element.212, bf16[768,2048]{1,0:T(8,128)(2,1)S(1)} %get-tuple-element.213), kind=kOutput, calls=%fused_computation.5 | convolution fusion | flops 3223322624 | bytes 8912896 | tf_op jit(solution)/shard_map/dot_general | solution.py:25
  (60 shorter events, 3.4 us)
Async XLA Ops:
  61.2 6.8 %copy-start.4 = (s32[32]{0:T(128)S(1)}, s32[32]{0:T(128)}, u32[]{:S(2)}) copy-start(s32[32]{0:T(128)} %param.15) | copy-start | bytes 388
  61.2 62.8 %all-to-all-start = ((bf16[32,32,2048]{2,1,0:T(8,128)(2,1)}), bf16[32,32,2048]{2,1,0:T(8,128)(2,1)}, u32[]{:S(2)}, u32[]{:S(2)}) async-start(bf16[32,32,2048]{2,1,0:T(8,128)(2,1)} %bitcast.35), calls=%async_computation | async-start | bytes 8388608 | tf_op jit(solution)/shard_map/all_to_all | solution.py:211
  124.0 61.6 %all-to-all-start.3 = ((bf16[32,64,1024]{2,1,0:T(8,128)(2,1)}), bf16[32,64,1024]{2,1,0:T(8,128)(2,1)}, u32[]{:S(2)}, u32[]{:S(2)}) async-start(bf16[32,64,1024]{2,1,0:T(8,128)(2,1)} %gather_fusion.1), calls=%async_computation.3 | async-start | bytes 8388608 | tf_op jit(solution)/shard_map/all_to_all | solution.py:217
  135.3 57.0 %copy-start.7 = (s32[4]{0:T(128)S(1)}, s32[4]{0:T(128)}, u32[]{:S(2)}) copy-start(s32[4]{0:T(128)} %constant.152.clone) | copy-start | bytes 52
  135.3 58.9 %copy-start.5 = (s32[32]{0:T(128)S(1)}, s32[32]{0:T(128)}, u32[]{:S(2)}) copy-start(s32[32]{0:T(128)} %param.14) | copy-start | bytes 388
  185.6 64.6 %all-to-all-start.1 = ((bf16[32,32,2048]{2,1,0:T(8,128)(2,1)}), bf16[32,32,2048]{2,1,0:T(8,128)(2,1)}, u32[]{:S(2)}, u32[]{:S(2)}) async-start(bf16[32,32,2048]{2,1,0:T(8,128)(2,1)} %gather_fusion), calls=%async_computation.1 | async-start | bytes 8388608 | tf_op jit(solution)/shard_map/all_to_all | solution.py:217
  201.5 52.8 %copy-start.1 = (bf16[1,768,1024]{2,1,0:T(8,128)(2,1)S(1)}, bf16[1,768,1024]{2,1,0:T(8,128)(2,1)}, u32[]{:S(2)}) copy-start(bf16[1,768,1024]{2,1,0:T(8,128)(2,1)} %param.9) | copy-start | bytes 4718596
  201.5 52.8 %copy-start.3 = (f32[1,1024]{1,0:T(1,128)S(1)}, f32[1,1024]{1,0:T(1,128)}, u32[]{:S(2)}) copy-start(f32[1,1024]{1,0:T(1,128)} %refs_1_.23) | copy-start | bytes 12292
  250.2 4.6 %copy-start = (bf16[2048,1024]{1,0:T(8,128)(2,1)S(1)}, bf16[2048,1024]{1,0:T(8,128)(2,1)}, u32[]{:S(2)}) copy-start(bf16[2048,1024]{1,0:T(8,128)(2,1)} %bitcast_select_fusion.refs_3_.refs_4_) | copy-start | bytes 12582916
  259.9 9.8 %collective-permute-start.1 = (bf16[192,1024]{1,0:T(8,128)(2,1)S(1)}, bf16[192,1024]{1,0:T(8,128)(2,1)S(1)}, u32[]{:S(2)}, u32[]{:S(2)}) collective-permute-start(bf16[192,1024]{1,0:T(8,128)(2,1)S(1)} %get-tuple-element.116), channel_id=1, source_target_pairs={{0,32},{1,33},{2,34},{3,35},{4,36},{5,37},{6,38},{7,39},{8,40},{9,... | collective-permute-start | bytes 1179656 | tf_op jit(solution)/shard_map/ppermute | solution.py:195
  266.3 10.7 %collective-permute-start = (bf16[192,1024]{1,0:T(8,128)(2,1)S(1)}, bf16[192,1024]{1,0:T(8,128)(2,1)S(1)}, u32[]{:S(2)}, u32[]{:S(2)}) collective-permute-start(bf16[192,1024]{1,0:T(8,128)(2,1)S(1)} %get-tuple-element.115), channel_id=1, source_target_pairs={{0,32},{1,33},{2,34},{3,35},{4,36},{5,37},{6,38},{7,39},{8,40},{9,... | collective-permute-start | bytes 1179656 | tf_op jit(solution)/shard_map/ppermute | solution.py:195
  274.9 10.6 %collective-permute-start.4 = (bf16[192,1024]{1,0:T(8,128)(2,1)S(1)}, bf16[192,1024]{1,0:T(8,128)(2,1)S(1)}, u32[]{:S(2)}, u32[]{:S(2)}) collective-permute-start(bf16[192,1024]{1,0:T(8,128)(2,1)S(1)} %get-tuple-element.128), channel_id=1, source_target_pairs={{0,32},{1,33},{2,34},{3,35},{4,36},{5,37},{6,38},{7,39},{8,40},{9,... | collective-permute-start | bytes 1179656 | tf_op jit(solution)/shard_map/ppermute | solution.py:195
  276.3 9.9 %collective-permute-start.3 = (bf16[192,1024]{1,0:T(8,128)(2,1)S(1)}, bf16[192,1024]{1,0:T(8,128)(2,1)S(1)}, u32[]{:S(2)}, u32[]{:S(2)}) collective-permute-start(bf16[192,1024]{1,0:T(8,128)(2,1)S(1)} %get-tuple-element.128), channel_id=1, source_target_pairs={{32,64},{33,65},{34,66},{35,67},{36,68},{37,69},{38,70},{39,71},{4... | collective-permute-start | bytes 1179656 | tf_op jit(solution)/shard_map/ppermute | solution.py:195
  282.0 4.2 %collective-permute-start.2 = (bf16[192,1024]{1,0:T(8,128)(2,1)S(1)}, bf16[192,1024]{1,0:T(8,128)(2,1)S(1)}, u32[]{:S(2)}, u32[]{:S(2)}) collective-permute-start(bf16[192,1024]{1,0:T(8,128)(2,1)S(1)} %get-tuple-element.127), channel_id=1, source_target_pairs={{0,32},{1,33},{2,34},{3,35},{4,36},{5,37},{6,38},{7,39},{8,40},{9,... | collective-permute-start | bytes 1179656 | tf_op jit(solution)/shard_map/ppermute | solution.py:195
  284.8 3.6 collective-permute-start.6
  286.8 5.7 %collective-permute-start.9 = (bf16[192,1024]{1,0:T(8,128)(2,1)S(1)}, bf16[192,1024]{1,0:T(8,128)(2,1)S(1)}, u32[]{:S(2)}, u32[]{:S(2)}) collective-permute-start(bf16[192,1024]{1,0:T(8,128)(2,1)S(1)} %get-tuple-element.139), channel_id=1, source_target_pairs={{64,96},{65,97},{66,98},{67,99},{68,100},{69,101},{70,102},{71,103... | collective-permute-start | bytes 1179656 | tf_op jit(solution)/shard_map/ppermute | solution.py:195
  287.5 5.0 %collective-permute-start.8 = (bf16[192,1024]{1,0:T(8,128)(2,1)S(1)}, bf16[192,1024]{1,0:T(8,128)(2,1)S(1)}, u32[]{:S(2)}, u32[]{:S(2)}) collective-permute-start(bf16[192,1024]{1,0:T(8,128)(2,1)S(1)} %get-tuple-element.146), channel_id=1, source_target_pairs={{32,64},{33,65},{34,66},{35,67},{36,68},{37,69},{38,70},{39,71},{4... | collective-permute-start | bytes 1179656 | tf_op jit(solution)/shard_map/ppermute | solution.py:195
  289.0 4.8 %collective-permute-start.7 = (bf16[192,1024]{1,0:T(8,128)(2,1)S(1)}, bf16[192,1024]{1,0:T(8,128)(2,1)S(1)}, u32[]{:S(2)}, u32[]{:S(2)}) collective-permute-start(bf16[192,1024]{1,0:T(8,128)(2,1)S(1)} %get-tuple-element.145), channel_id=1, source_target_pairs={{64,96},{65,97},{66,98},{67,99},{68,100},{69,101},{70,102},{71,103... | collective-permute-start | bytes 1179656 | tf_op jit(solution)/shard_map/ppermute | solution.py:195
  289.7 4.1 %collective-permute-start.5 = (bf16[192,1024]{1,0:T(8,128)(2,1)S(1)}, bf16[192,1024]{1,0:T(8,128)(2,1)S(1)}, u32[]{:S(2)}, u32[]{:S(2)}) collective-permute-start(bf16[192,1024]{1,0:T(8,128)(2,1)S(1)} %get-tuple-element.139), channel_id=1, source_target_pairs={{32,64},{33,65},{34,66},{35,67},{36,68},{37,69},{38,70},{39,71},{4... | collective-permute-start | bytes 1179656 | tf_op jit(solution)/shard_map/ppermute | solution.py:195
  293.2 4.9 %collective-permute-start.11 = (bf16[192,1024]{1,0:T(8,128)(2,1)S(1)}, bf16[192,1024]{1,0:T(8,128)(2,1)S(1)}, u32[]{:S(2)}, u32[]{:S(2)}) collective-permute-start(bf16[192,1024]{1,0:T(8,128)(2,1)S(1)} %get-tuple-element.158), channel_id=1, source_target_pairs={{64,96},{65,97},{66,98},{67,99},{68,100},{69,101},{70,102},{71,103... | collective-permute-start | bytes 1179656 | tf_op jit(solution)/shard_map/ppermute | solution.py:195
  293.9 2.1 copy-start.6
  294.5 5.3 %collective-permute-start.10 = (bf16[192,1024]{1,0:T(8,128)(2,1)S(1)}, bf16[192,1024]{1,0:T(8,128)(2,1)S(1)}, u32[]{:S(2)}, u32[]{:S(2)}) collective-permute-start(bf16[192,1024]{1,0:T(8,128)(2,1)S(1)} %get-tuple-element.157), channel_id=1, source_target_pairs={{64,96},{65,97},{66,98},{67,99},{68,100},{69,101},{70,102},{71,103... | collective-permute-start | bytes 1179656 | tf_op jit(solution)/shard_map/ppermute | solution.py:195
  299.8 1.4 copy-start.2
  301.8 3.5 collective-permute-start.13
  303.1 4.3 %collective-permute-start.12 = (bf16[192,1024]{1,0:T(8,128)(2,1)S(1)}, bf16[192,1024]{1,0:T(8,128)(2,1)S(1)}, u32[]{:S(2)}, u32[]{:S(2)}) collective-permute-start(bf16[192,1024]{1,0:T(8,128)(2,1)S(1)} %get-tuple-element.175), channel_id=1, source_target_pairs={{96,64},{97,65},{98,66},{99,67},{100,68},{101,69},{102,70},{103,71... | collective-permute-start | bytes 1179656 | tf_op jit(solution)/shard_map/ppermute | solution.py:195
  306.7 5.5 %collective-permute-start.17 = (bf16[192,1024]{1,0:T(8,128)(2,1)S(1)}, bf16[192,1024]{1,0:T(8,128)(2,1)S(1)}, u32[]{:S(2)}, u32[]{:S(2)}) collective-permute-start(bf16[192,1024]{1,0:T(8,128)(2,1)S(1)} %get-tuple-element.184), channel_id=1, source_target_pairs={{96,64},{97,65},{98,66},{99,67},{100,68},{101,69},{102,70},{103,71... | collective-permute-start | bytes 1179656 | tf_op jit(solution)/shard_map/ppermute | solution.py:195
  308.0 4.8 %collective-permute-start.16 = (bf16[192,1024]{1,0:T(8,128)(2,1)S(1)}, bf16[192,1024]{1,0:T(8,128)(2,1)S(1)}, u32[]{:S(2)}, u32[]{:S(2)}) collective-permute-start(bf16[192,1024]{1,0:T(8,128)(2,1)S(1)} %get-tuple-element.183), channel_id=1, source_target_pairs={{96,64},{97,65},{98,66},{99,67},{100,68},{101,69},{102,70},{103,71... | collective-permute-start | bytes 1179656 | tf_op jit(solution)/shard_map/ppermute | solution.py:195
  308.7 4.1 %collective-permute-start.15 = (bf16[192,1024]{1,0:T(8,128)(2,1)S(1)}, bf16[192,1024]{1,0:T(8,128)(2,1)S(1)}, u32[]{:S(2)}, u32[]{:S(2)}) collective-permute-start(bf16[192,1024]{1,0:T(8,128)(2,1)S(1)} %get-tuple-element.184), channel_id=1, source_target_pairs={{64,32},{65,33},{66,34},{67,35},{68,36},{69,37},{70,38},{71,39},{7... | collective-permute-start | bytes 1179656 | tf_op jit(solution)/shard_map/ppermute | solution.py:195
  311.5 4.0 %collective-permute-start.14 = (bf16[192,1024]{1,0:T(8,128)(2,1)S(1)}, bf16[192,1024]{1,0:T(8,128)(2,1)S(1)}, u32[]{:S(2)}, u32[]{:S(2)}) collective-permute-start(bf16[192,1024]{1,0:T(8,128)(2,1)S(1)} %get-tuple-element.183), channel_id=1, source_target_pairs={{64,32},{65,33},{66,34},{67,35},{68,36},{69,37},{70,38},{71,39},{7... | collective-permute-start | bytes 1179656 | tf_op jit(solution)/shard_map/ppermute | solution.py:195
  313.4 41.4 %collective-permute-start.20 = (bf16[192,1024]{1,0:T(8,128)(2,1)S(1)}, bf16[192,1024]{1,0:T(8,128)(2,1)S(1)}, u32[]{:S(2)}, u32[]{:S(2)}) collective-permute-start(bf16[192,1024]{1,0:T(8,128)(2,1)S(1)} %get-tuple-element.195), channel_id=1, source_target_pairs={{32,0},{33,1},{34,2},{35,3},{36,4},{37,5},{38,6},{39,7},{40,8},{41... | collective-permute-start | bytes 1179656 | tf_op jit(solution)/shard_map/ppermute | solution.py:195
  314.7 40.1 %collective-permute-start.21 = (bf16[192,1024]{1,0:T(8,128)(2,1)S(1)}, bf16[192,1024]{1,0:T(8,128)(2,1)S(1)}, u32[]{:S(2)}, u32[]{:S(2)}) collective-permute-start(bf16[192,1024]{1,0:T(8,128)(2,1)S(1)} %get-tuple-element.196), channel_id=1, source_target_pairs={{64,32},{65,33},{66,34},{67,35},{68,36},{69,37},{70,38},{71,39},{7... | collective-permute-start | bytes 1179656 | tf_op jit(solution)/shard_map/ppermute | solution.py:195
  316.3 46.6 %collective-permute-start.18 = (bf16[192,1024]{1,0:T(8,128)(2,1)S(1)}, bf16[192,1024]{1,0:T(8,128)(2,1)S(1)}, u32[]{:S(2)}, u32[]{:S(2)}) collective-permute-start(bf16[192,1024]{1,0:T(8,128)(2,1)S(1)} %get-tuple-element.194), channel_id=1, source_target_pairs={{32,0},{33,1},{34,2},{35,3},{36,4},{37,5},{38,6},{39,7},{40,8},{41... | collective-permute-start | bytes 1179656 | tf_op jit(solution)/shard_map/ppermute | solution.py:195
  317.6 45.3 %collective-permute-start.19 = (bf16[192,1024]{1,0:T(8,128)(2,1)S(1)}, bf16[192,1024]{1,0:T(8,128)(2,1)S(1)}, u32[]{:S(2)}, u32[]{:S(2)}) collective-permute-start(bf16[192,1024]{1,0:T(8,128)(2,1)S(1)} %get-tuple-element.195), channel_id=1, source_target_pairs={{64,32},{65,33},{66,34},{67,35},{68,36},{69,37},{70,38},{71,39},{7... | collective-permute-start | bytes 1179656 | tf_op jit(solution)/shard_map/ppermute | solution.py:195
  360.0 12.2 %collective-permute-start.23 = (bf16[192,1024]{1,0:T(8,128)(2,1)S(1)}, bf16[192,1024]{1,0:T(8,128)(2,1)S(1)}, u32[]{:S(2)}, u32[]{:S(2)}) collective-permute-start(bf16[192,1024]{1,0:T(8,128)(2,1)S(1)} %get-tuple-element.204), channel_id=1, source_target_pairs={{32,0},{33,1},{34,2},{35,3},{36,4},{37,5},{38,6},{39,7},{40,8},{41... | collective-permute-start | bytes 1179656 | tf_op jit(solution)/shard_map/ppermute | solution.py:195
  368.1 10.6 %collective-permute-start.22 = (bf16[192,1024]{1,0:T(8,128)(2,1)S(1)}, bf16[192,1024]{1,0:T(8,128)(2,1)S(1)}, u32[]{:S(2)}, u32[]{:S(2)}) collective-permute-start(bf16[192,1024]{1,0:T(8,128)(2,1)S(1)} %get-tuple-element.203), channel_id=1, source_target_pairs={{32,0},{33,1},{34,2},{35,3},{36,4},{37,5},{38,6},{39,7},{40,8},{41... | collective-permute-start | bytes 1179656 | tf_op jit(solution)/shard_map/ppermute | solution.py:195
